TPU v7x, 16 devices: a whole 2x2x2 slice. The times are simulated.
16 devices in a mesh: data: 16 (over z, y, x, core).
Axes of the slice: x: 2, y: 2, z: 2, core: 2. Of those that a mesh axis runs over, the one named last changes fastest.
Arguments:
- act_in: bfloat16 [65536, 896], P('data')
- grad_out: bfloat16 [65536, 896], P('data')
- w_up1: bfloat16 [896, 4864], replicated
- w_down1: bfloat16 [4864, 896], replicated
- w_up2: bfloat16 [896, 4864], replicated
- w_down2: bfloat16 [4864, 896], replicated
- master_up1: float32 [896, 4864], P('data')
- master_down1: float32 [4864, 896], P('data')
- master_up2: float32 [896, 4864], P('data')
- master_down2: float32 [4864, 896], P('data')
- mom_up1: float32 [896, 4864], P('data')
- mom_down1: float32 [4864, 896], P('data')
- mom_up2: float32 [896, 4864], P('data')
- mom_down2: float32 [4864, 896], P('data')
- vel_up1: float32 [896, 4864], P('data')
- vel_down1: float32 [4864, 896], P('data')
- vel_up2: float32 [896, 4864], P('data')
- vel_down2: float32 [4864, 896], P('data')
- learn_rate: float32 [], replicated
- clip_norm: float32 [], replicated
Outputs:
- output 1: bfloat16 [896, 4864], replicated
- output 2: bfloat16 [4864, 896], replicated
- output 3: bfloat16 [896, 4864], replicated
- output 4: bfloat16 [4864, 896], replicated
- output 5: float32 [896, 4864], P('data')
- output 6: float32 [4864, 896], P('data')
- output 7: float32 [896, 4864], P('data')
- output 8: float32 [4864, 896], P('data')
- output 9: float32 [896, 4864], P('data')
- output 10: float32 [4864, 896], P('data')
- output 11: float32 [896, 4864], P('data')
- output 12: float32 [4864, 896], P('data')
- output 13: float32 [896, 4864], P('data')
- output 14: float32 [4864, 896], P('data')
- output 15: float32 [896, 4864], P('data')
- output 16: float32 [4864, 896], P('data')
- output 17: float32 [], replicated
All inputs are finite; a program needn't handle non-finite values.
Results may differ from a plain program's by a relative error of at most 0.010218.
Values are sent between devices in bfloat16 or wider.
A program may use at most 1 GiB of HBM per device.

v0:
```python
import math
import jax
import jax.numpy as jnp
from jax import lax
from jax.sharding import PartitionSpec as P, NamedSharding

STEP = 20
BETA_ONE = 0.9
BETA_TWO = 0.95
EPSILON = 1e-8
NORM_EPS = 1e-6
CORR_ONE = 1.0 - BETA_ONE ** STEP
CORR_TWO = 1.0 - BETA_TWO ** STEP
ROOT_HALF = math.sqrt(0.5)
INV_ROOT_TAU = 1.0 / math.sqrt(2.0 * math.pi)


def mat_nt(left, right):
    return lax.dot_general(left, right, (((1,), (1,)), ((), ())), preferred_element_type=jnp.float32)


def mat_tn(left, right):
    return lax.dot_general(left, right, (((0,), (0,)), ((), ())), preferred_element_type=jnp.float32)


def gelu_pair(pre):
    normal_cdf = 0.5 * (1.0 + lax.erf(pre * ROOT_HALF))
    density = jnp.exp(-0.5 * pre * pre) * INV_ROOT_TAU
    return pre * normal_cdf, normal_cdf + pre * density


def fwd_bwd(rows_in, rows_grad, w_up1, w_down1, w_up2, w_down2):
    pre_up1 = jnp.dot(rows_in, w_up1, preferred_element_type=jnp.float32)
    gel_up1, der_up1 = gelu_pair(pre_up1)
    act_up1 = gel_up1.astype(jnp.bfloat16)
    mid_act = jnp.dot(act_up1, w_down1, preferred_element_type=jnp.float32).astype(jnp.bfloat16)
    pre_up2 = jnp.dot(mid_act, w_up2, preferred_element_type=jnp.float32)
    gel_up2, der_up2 = gelu_pair(pre_up2)
    act_up2 = gel_up2.astype(jnp.bfloat16)
    grad_act2 = mat_nt(rows_grad, w_down2).astype(jnp.bfloat16)
    grad_pre2 = (grad_act2.astype(jnp.float32) * der_up2).astype(jnp.bfloat16)
    grad_mid = mat_nt(grad_pre2, w_up2).astype(jnp.bfloat16)
    grad_act1 = mat_nt(grad_mid, w_down1).astype(jnp.bfloat16)
    grad_pre1 = (grad_act1.astype(jnp.float32) * der_up1).astype(jnp.bfloat16)
    return ((act_up2, rows_grad), (mid_act, grad_pre2), (act_up1, grad_mid), (rows_in, grad_pre1))


def adam_step(grad_rows, master_old, mom_old, vel_old, clip_scale, learn_rate):
    scaled = clip_scale * grad_rows
    mom_new = BETA_ONE * mom_old + (1.0 - BETA_ONE) * scaled
    vel_new = BETA_TWO * vel_old + (1.0 - BETA_TWO) * scaled * scaled
    master_new = master_old - learn_rate * (mom_new / CORR_ONE) / (jnp.sqrt(vel_new / CORR_TWO) + EPSILON)
    return master_new.astype(jnp.bfloat16), master_new, mom_new, vel_new


def solution(mesh):
    groups = mesh.shape["data"]
    rows_spec = P("data", None)
    full_spec = P(None, None)
    scalar_spec = P()

    def shard_body(act_in, grad_out, w_up1, w_down1, w_up2, w_down2, master_up1, master_down1, master_up2, master_down2, mom_up1, mom_down1, mom_up2, mom_down2, vel_up1, vel_down1, vel_up2, vel_down2, learn_rate, clip_norm):
        grad_pairs = fwd_bwd(act_in, grad_out, w_up1, w_down1, w_up2, w_down2)
        shards = []
        for layer_in, layer_delta in grad_pairs:
            local_grad = mat_tn(layer_in, layer_delta)
            shards.append(lax.psum_scatter(local_grad, "data", scatter_dimension=0, tiled=True) / groups)
        grad_list = shards[::-1]
        local_sq = sum(jnp.sum(grad_rows * grad_rows) for grad_rows in grad_list)
        grad_norm = jnp.sqrt(lax.psum(local_sq, "data"))
        clip_scale = jnp.minimum(1.0, clip_norm / (grad_norm + NORM_EPS))
        master_list = (master_up1, master_down1, master_up2, master_down2)
        mom_list = (mom_up1, mom_down1, mom_up2, mom_down2)
        vel_list = (vel_up1, vel_down1, vel_up2, vel_down2)
        layer_states = [adam_step(grad_list[layer_idx], master_list[layer_idx], mom_list[layer_idx], vel_list[layer_idx], clip_scale, learn_rate) for layer_idx in range(4)]
        new_weights = [lax.all_gather(layer_state[0], "data", axis=0, tiled=True) for layer_state in layer_states]
        results = new_weights
        for field_idx in range(1, 4):
            results = results + [layer_state[field_idx] for layer_state in layer_states]
        return tuple(results + [grad_norm])

    in_specs = (rows_spec, rows_spec) + (full_spec,) * 4 + (rows_spec,) * 12 + (scalar_spec, scalar_spec)
    out_specs = (full_spec,) * 4 + (rows_spec,) * 12 + (scalar_spec,)
    return jax.shard_map(shard_body, mesh=mesh, in_specs=in_specs, out_specs=out_specs, check_vma=False)
```

profile of v0, /device:TPU:0, one launch (start us, length us, event | category | flops | bytes accessed | tf_op | source)
XLA Modules:
  0.0 1430.7 jit_solution(17083988175645864259)
XLA Ops:
  7.2 0.0 reduce-scatter.13.cloned.1.call-start
  7.2 55.4 %multiply_convert_fusion.1 = (bf16[4096,4864]{1,0:T(8,128)(2,1)}, f32[4096,4864]{1,0:T(8,128)}) fusion(bf16[4096,896]{1,0:T(8,128)(2,1)} %param.20, bf16[896,4864]{1,0:T(8,128)(2,1)} %param.22), kind=kOutput, calls=%fused_computation.16 | convolution fusion | flops 35801530368 | bytes 135593984 | tf_op jit(solution)/shard_map/dot_general | solution.py:33
  62.7 46.8 %convolution_convert_fusion.1 = bf16[4096,896]{1,0:T(8,128)(2,1)} fusion(bf16[4096,4864]{1,0:T(8,128)(2,1)} %get-tuple-element.67, bf16[4864,896]{1,0:T(8,128)(2,1)S(1)} %copy-done.5), kind=kOutput, calls=%fused_computation.22 | convolution fusion | flops 35705585664 | bytes 55902208 | tf_op jit(solution)/shard_map/dot_general | solution.py:36
  109.5 47.9 %fusion.32 = f32[4096,4864]{1,0:T(8,128)} fusion(bf16[4096,896]{1,0:T(8,128)(2,1)} %convolution_convert_fusion.1, bf16[896,4864]{1,0:T(8,128)(2,1)S(1)} %copy-done.4), kind=kOutput, calls=%fused_computation.49 | convolution fusion | flops 35701915648 | bytes 95748096 | tf_op jit(solution)/shard_map/dot_general | solution.py:37
  157.4 68.4 %fusion.5 = bf16[4096,4864]{1,0:T(8,128)(2,1)} fusion(f32[4096,4864]{1,0:T(8,128)} %fusion.32, bf16[4096,896]{1,0:T(8,128)(2,1)} %param.21, bf16[4864,896]{1,0:T(8,128)(2,1)} %param.25), kind=kOutput, calls=%fused_computation.7 | convolution fusion | flops 35940990976 | bytes 135593984 | tf_op jit(solution)/shard_map/dot_general | solution.py:19
  225.8 49.3 %convolution_convert_fusion = bf16[4096,896]{1,0:T(8,128)(2,1)} fusion(bf16[4096,4864]{1,0:T(8,128)(2,1)} %fusion.5, bf16[896,4864]{1,0:T(8,128)(2,1)} %param.24), kind=kOutput, calls=%fused_computation.21 | convolution fusion | flops 35705585664 | bytes 55902208 | tf_op jit(solution)/shard_map/dot_general | solution.py:19
  275.1 49.6 %fusion.33 = bf16[4096,4864]{1,0:T(8,128)(2,1)} fusion(bf16[4096,896]{1,0:T(8,128)(2,1)} %convolution_convert_fusion, bf16[4864,896]{1,0:T(8,128)(2,1)} %param.23), kind=kOutput, calls=%fused_computation.50 | convolution fusion | flops 35701915648 | bytes 55902208 | tf_op jit(solution)/shard_map/dot_general | solution.py:19
  324.7 60.4 %fusion.15 = f32[896,4864]{0,1:T(8,128)} fusion(bf16[4096,896]{1,0:T(8,128)(2,1)} %param.20, f32[4096,4864]{1,0:T(8,128)} %get-tuple-element.68, bf16[4096,4864]{1,0:T(8,128)(2,1)} %fusion.33), kind=kOutput, calls=%fused_computation.20 | convolution fusion | flops 35921068032 | bytes 144310272 | tf_op jit(solution)/shard_map/dot_general | solution.py:23
  385.0 18.9 %copy.71 = f32[896,4864]{1,0:T(8,128)} copy(f32[896,4864]{0,1:T(8,128)} %fusion.15) | data formatting | bytes 34865152
  404.0 0.0 reduce-scatter.13.cloned.1.call-update
  404.0 0.0 reduce-scatter.9.cloned.1.call-start
  404.0 62.0 %fusion.34 = f32[4864,896]{1,0:T(8,128)} fusion(bf16[4096,4864]{1,0:T(8,128)(2,1)} %get-tuple-element.67, bf16[4096,896]{1,0:T(8,128)(2,1)} %convolution_convert_fusion), kind=kOutput, calls=%fused_computation.51 | convolution fusion | flops 35701915648 | bytes 64618496 | tf_op jit(solution)/shard_map/dot_general | solution.py:23
  466.1 0.0 reduce-scatter.9.cloned.1.call-update
  466.1 0.0 reduce-scatter.15.cloned.1.call-start
  466.1 46.3 %fusion.35 = f32[896,4864]{1,0:T(8,128)} fusion(bf16[4096,896]{1,0:T(8,128)(2,1)} %convolution_convert_fusion.1, bf16[4096,4864]{1,0:T(8,128)(2,1)} %fusion.5), kind=kOutput, calls=%fused_computation.52 | convolution fusion | flops 35701915648 | bytes 64618496
  512.5 0.0 reduce-scatter.15.cloned.1.call-update
  512.5 0.0 reduce-scatter.11.cloned.1.call-start
  512.5 50.8 %fusion.12 = f32[4864,896]{1,0:T(8,128)} fusion(bf16[4096,896]{1,0:T(8,128)(2,1)} %param.21, f32[4096,4864]{1,0:T(8,128)} %fusion.32), kind=kOutput, calls=%fused_computation.18 | convolution fusion | flops 35801530368 | bytes 104464384 | tf_op jit(solution)/shard_map/dot_general | solution.py:23
  563.4 0.0 reduce-scatter.11.cloned.1.call-update
  563.4 0.0 all-gather.9.cloned.1.call-start
  564.7 26.1 %reduce-scatter.13.cloned.1.call-done = f32[56,4864]{1,0:T(8,128)} async-done(((f32[896,4864]{1,0:T(8,128)}), f32[56,4864]{1,0:T(8,128)}) %reduce-scatter.13.cloned.1.call-update) | async-done | bytes 1089552 | tf_op jit(solution)/shard_map/reduce_scatter | solution.py:67
  590.9 1.9 copy.72
  592.8 182.5 %reduce-scatter.9.cloned.1.call-done = f32[304,896]{1,0:T(8,128)} async-done(((f32[4864,896]{1,0:T(8,128)}), f32[304,896]{1,0:T(8,128)}) %reduce-scatter.9.cloned.1.call-update) | async-done | bytes 1089552 | tf_op jit(solution)/shard_map/reduce_scatter | solution.py:67
  775.3 2.1 multiply_reduce_fusion.3
  777.4 1.2 multiply_reduce_fusion.1
  780.0 179.8 %reduce-scatter.15.cloned.1.call-done = f32[56,4864]{1,0:T(8,128)} async-done(((f32[896,4864]{1,0:T(8,128)}), f32[56,4864]{1,0:T(8,128)}) %reduce-scatter.15.cloned.1.call-update) | async-done | bytes 1089552 | tf_op jit(solution)/shard_map/reduce_scatter | solution.py:67
  959.7 1.9 copy.74
  961.6 1.2 multiply_reduce_fusion
  963.5 180.5 %reduce-scatter.11.cloned.1.call-done = f32[304,896]{1,0:T(8,128)} async-done(((f32[4864,896]{1,0:T(8,128)}), f32[304,896]{1,0:T(8,128)}) %reduce-scatter.11.cloned.1.call-update) | async-done | bytes 1089552 | tf_op jit(solution)/shard_map/reduce_scatter | solution.py:67
  1144.0 2.2 multiply_reduce_fusion.2
  1146.9 31.2 %psum.7 = f32[]{:T(128)} all-reduce(f32[]{:T(128)S(6)} %add.76), channel_id=1, replica_groups=mesh['data'=16] {'data'}, use_global_device_ids=true, to_apply=%region_8.0 | all-reduce | flops 1 | bytes 8 | tf_op jit(solution)/shard_map/psum | solution.py:70
  1178.8 4.6 fusion.26
  1183.4 0.0 all-gather.9.cloned.1.call-update
  1183.5 0.0 all-gather.11.cloned.1.call-start
  1183.5 4.3 fusion.24
  1187.8 0.0 all-gather.11.cloned.1.call-update
  1187.8 0.0 all-gather.7.cloned.1.call-start
  1187.9 4.3 fusion.28
  1192.2 0.0 all-gather.5.cloned.1.call-start
  1192.3 3.9 fusion.30
  1196.2 38.0 %all-gather.9.cloned.1.call-done = bf16[896,4864]{1,0:T(8,128)(2,1)} async-done(((bf16[56,4864]{1,0:T(8,128)(2,1)}), bf16[896,4864]{1,0:T(8,128)(2,1)}) %all-gather.9.cloned.1.call-update) | async-done | bytes 8716304 | tf_op jit(solution)/shard_map/all_gather | solution.py:76
  1234.2 52.5 %all-gather.11.cloned.1.call-done = bf16[4864,896]{1,0:T(8,128)(2,1)} async-done(((bf16[304,896]{1,0:T(8,128)(2,1)}), bf16[4864,896]{1,0:T(8,128)(2,1)}) %all-gather.11.cloned.1.call-update) | async-done | bytes 8716304 | tf_op jit(solution)/shard_map/all_gather | solution.py:76
  1286.7 52.6 %all-gather.7.cloned.1.call-done = bf16[4864,896]{1,0:T(8,128)(2,1)} async-done(((bf16[304,896]{1,0:T(8,128)(2,1)}), bf16[4864,896]{1,0:T(8,128)(2,1)}) %all-gather.7.cloned.1.call-update) | async-done | bytes 8716304 | tf_op jit(solution)/shard_map/all_gather | solution.py:76
  1339.2 52.6 %all-gather.5.cloned.1.call-done = bf16[896,4864]{1,0:T(8,128)(2,1)} async-done(((bf16[56,4864]{1,0:T(8,128)(2,1)}), bf16[896,4864]{1,0:T(8,128)(2,1)}) %all-gather.5.cloned.1.call-update) | async-done | bytes 8716304 | tf_op jit(solution)/shard_map/all_gather | solution.py:76
  1391.8 7.5 copy.81
  1399.4 7.7 copy.82
  1407.1 7.5 copy.83
  1414.6 7.7 copy.84
  (14 shorter events, 0.1 us)
Async XLA Ops:
  7.2 583.7 %reduce-scatter.13.cloned.1.call-start = ((), (), s32[]{:S(2)}) async-start(), calls=%async_computation.10 | async-start | bytes 18522112 | tf_op jit(solution)/shard_map/reduce_scatter | solution.py:67
  7.2 55.5 %copy-start.5 = (bf16[4864,896]{1,0:T(8,128)(2,1)S(1)}, bf16[4864,896]{1,0:T(8,128)(2,1)}, u32[]{:S(2)}) copy-start(bf16[4864,896]{1,0:T(8,128)(2,1)} %param.23) | copy-start | bytes 26148868
  62.7 46.8 %copy-start.4 = (bf16[896,4864]{1,0:T(8,128)(2,1)S(1)}, bf16[896,4864]{1,0:T(8,128)(2,1)}, u32[]{:S(2)}) copy-start(bf16[896,4864]{1,0:T(8,128)(2,1)} %param.24) | copy-start | bytes 26148868
  404.0 371.3 %reduce-scatter.9.cloned.1.call-start = ((), (), s32[]{:S(2)}) async-start(), calls=%async_computation.4 | async-start | bytes 18522112 | tf_op jit(solution)/shard_map/reduce_scatter | solution.py:67
  466.1 493.7 %reduce-scatter.15.cloned.1.call-start = ((), (), s32[]{:S(2)}) async-start(), calls=%async_computation.11 | async-start | bytes 18522112 | tf_op jit(solution)/shard_map/reduce_scatter | solution.py:67
  512.5 631.5 %reduce-scatter.11.cloned.1.call-start = ((), (), s32[]{:S(2)}) async-start(), calls=%async_computation.5 | async-start | bytes 18522112 | tf_op jit(solution)/shard_map/reduce_scatter | solution.py:67
  563.4 670.8 %all-gather.9.cloned.1.call-start = ((), (), s32[]{:S(2)}) async-start(), calls=%async_computation.8 | async-start | bytes 9261056 | tf_op jit(solution)/shard_map/all_gather | solution.py:76
  1144.0 39.5 %copy-start.2 = (f32[304,896]{1,0:T(8,128)S(1)}, f32[304,896]{1,0:T(8,128)}, u32[]{:S(2)}) copy-start(f32[304,896]{1,0:T(8,128)} %reduce-scatter.11.cloned.1.call-done) | copy-start | bytes 3268612
  1178.8 9.1 copy-start.1
  1183.4 8.8 copy-start
  1183.5 103.2 %all-gather.11.cloned.1.call-start = ((), (), s32[]{:S(2)}) async-start(), calls=%async_computation.9 | async-start | bytes 9261056 | tf_op jit(solution)/shard_map/all_gather | solution.py:76
  1187.8 4.5 copy-start.3
  1187.8 151.4 %all-gather.7.cloned.1.call-start = ((), (), s32[]{:S(2)}) async-start(), calls=%async_computation.7 | async-start | bytes 9261056 | tf_op jit(solution)/shard_map/all_gather | solution.py:76
  1192.2 199.6 %all-gather.5.cloned.1.call-start = ((), (), s32[]{:S(2)}) async-start(), calls=%async_computation.6 | async-start | bytes 9261056 | tf_op jit(solution)/shard_map/all_gather | solution.py:76
Sparse Core Ops, SparseCore 0:
  404.1 186.7 reduce-scatter.12
  593.2 182.0 reduce-scatter.8
  777.6 182.1 reduce-scatter.14
  961.9 182.0 reduce-scatter.10
  1183.6 50.5 all-gather.8
  1236.9 49.7 all-gather.10
  1289.5 49.7 all-gather.6
  1342.0 49.7 all-gather.4
where the time goes:
time: 1440 us; the launch traced here: 1430 us
  waiting for transfers between devices  765 us (53%)
  matrix products  537 us (37%)
  local copies, waits for them, and re-layouts  53.1 us (4%)
  blocking collectives  31.2 us (2%)
  other arithmetic  23.9 us (2%)
  between operations  20.5 us (1%)
    reduce_scatter x4, waiting for transfers between devices, shard_body(): lax.psum_scatter(local_grad, 'data', scatter_dimension=0, tiled=True)  569 us
    all_gather x4, waiting for transfers between devices, shard_body(): lax.all_gather(layer_state[0], 'data', axis=0, tiled=True)  196 us
    dot_general x3, matrix products, mat_tn(): lax.dot_general(left, right, (((0,), (0,)), ((), ())), preferred_element_...  173 us
    dot_general x3, matrix products, mat_nt(): lax.dot_general(left, right, (((1,), (1,)), ((), ())), preferred_element_...  167 us
    dot_general x1, matrix products, fwd_bwd(): pre_up1 = jnp.dot(rows_in, w_up1, preferred_element_type=jnp.float32)  55.4 us
    unnamed x19, local copies, waits for them, and re-layouts  53.1 us
    dot_general x1, matrix products, fwd_bwd(): pre_up2 = jnp.dot(mid_act, w_up2, preferred_element_type=jnp.float32)  47.9 us
    dot_general x1, matrix products, fwd_bwd(): jnp.dot(act_up1, w_down1, preferred_element_type=jnp.float32)  46.8 us
  transfers between devices with their start and end apart: 8, of which 8 were waited for; matrix products, arithmetic and copies ran while one was open for 13% of the time, Pallas kernels for 0%

commit v1 on v0

v1 whole, which is shorter than its diff:
```python
import functools
import math
import jax
import jax.numpy as jnp
from jax import lax
from jax.experimental import pallas as pl
from jax.experimental.pallas import tpu as pltpu
from jax.sharding import PartitionSpec as P

ROOT_HALF = math.sqrt(0.5)
INV_ROOT_TAU = 1.0 / math.sqrt(2.0 * math.pi)
F32, BF16 = jnp.float32, jnp.bfloat16
ANY = pl.BlockSpec(memory_space=pl.ANY)
HBM = pl.BlockSpec(memory_space=pltpu.HBM)

def dot_nn(a, b):
    return lax.dot_general(a, b, (((1,), (0,)), ((), ())), preferred_element_type=F32)
def dot_nt(a, b):
    return lax.dot_general(a, b, (((1,), (1,)), ((), ())), preferred_element_type=F32)

def gelu(z):
    return z * (0.5 * (1.0 + lax.erf(z * ROOT_HALF)))

def kernel_a(cfg, x_hbm, w1_hbm, w2_hbm, z_hbm, u_hbm, ut_hbm, xt_hbm,
             x_v, uacc, zout, w1, w2, h0, h1, sq, sqt, xsem, wsem, zsem, osem):
    nt, nr, rb, ft, d, nd = cfg
    hb = (h0, h1)
    xc = pltpu.make_async_copy(x_hbm, x_v, xsem.at[0])
    xc.start()

    def wcopies(j, slot):
        return (pltpu.make_async_copy(w1_hbm.at[j], w1.at[slot], wsem.at[slot]),
                pltpu.make_async_copy(w2_hbm.at[:, j], w2.at[slot], wsem.at[2 + slot]))
    for c in wcopies(0, 0):
        c.start()
    h1[...] = jnp.zeros_like(h1)
    def zero(r, _):
        uacc[pl.ds(pl.multiple_of(r * rb, rb), rb), :] = jnp.zeros((rb, d), F32)
        return 0
    lax.fori_loop(0, nr, zero, 0)
    xc.wait()
    for c in wcopies(0, 0):
        c.wait()
    zout[0, 0:rb, :] = dot_nn(x_v[0:rb, :], w1[0])

    def tile(j, _):
        slot = lax.rem(j, 2)
        nslot = lax.rem(j + 1, 2)
        pslot = lax.rem(jnp.maximum(j - 1, 0), 2)
        jn = jnp.minimum(j + 1, nt - 1)
        for r in range(nr):
            rows = pl.ds(r * rb, rb)
            pr = (r - 1) % nr
            prow = pl.ds(pr * rb, rb)
            w2p = w2[pslot if r == 0 else slot].reshape(ft, d)
            uacc[prow, :] += dot_nn(hb[(r + 1) % 2][...], w2p)
            if r == 0:
                for c in wcopies(jn, nslot):
                    c.start()
            if r == nr - 1:
                for c in wcopies(jn, nslot):
                    c.wait()
                @pl.when(j >= 1)
                def _():
                    pltpu.make_async_copy(zout.at[nslot], z_hbm.at[jn], zsem.at[nslot]).wait()
            hb[r % 2][...] = gelu(zout[slot, rows, :]).astype(BF16)
            if r < nr - 1:
                zout[slot, pl.ds((r + 1) * rb, rb), :] = dot_nn(x_v[pl.ds((r + 1) * rb, rb), :], w1[slot])
            else:
                zout[nslot, 0:rb, :] = dot_nn(x_v[0:rb, :], w1[nslot])
        pltpu.make_async_copy(zout.at[slot], z_hbm.at[j], zsem.at[slot]).start()
        return 0
    lax.fori_loop(0, nt, tile, 0)
    last = (nt - 1) % 2
    prow = pl.ds((nr - 1) * rb, rb)
    uacc[prow, :] += dot_nn(hb[(nr - 1) % 2][...], w2[last].reshape(ft, d))
    pltpu.make_async_copy(zout.at[last], z_hbm.at[nt - 1], zsem.at[last]).wait()
    def fin(r, _):
        rows = pl.ds(pl.multiple_of(r * rb, rb), rb)
        s = lax.rem(r, 2)
        cps = lambda: (pltpu.make_async_copy(sq.at[s], u_hbm.at[rows, :], osem.at[s]),
               pltpu.make_async_copy(sqt.at[s, 0], ut_hbm.at[:, rows], osem.at[2 + s]),
               pltpu.make_async_copy(sqt.at[s, 1], xt_hbm.at[:, rows], osem.at[4 + s]))
        @pl.when(r >= 2)
        def _():
            for c in cps():
                c.wait()
        v = uacc[rows, :].astype(BF16)
        sq[s] = v
        sqt[s, 0] = v.T
        sqt[s, 1] = x_v[rows, :].T
        for c in cps():
            c.start()
        return 0
    lax.fori_loop(0, nr, fin, 0)
    for s in range(2):
        rows = pl.ds((nr - 2 + s) * rb, rb)
        for c in (pltpu.make_async_copy(sq.at[s], u_hbm.at[rows, :], osem.at[s]),
               pltpu.make_async_copy(sqt.at[s, 0], ut_hbm.at[:, rows], osem.at[2 + s]),
               pltpu.make_async_copy(sqt.at[s, 1], xt_hbm.at[:, rows], osem.at[4 + s])):
            c.wait()

def forward_one(x, w1p, w2r):
    t, d = x.shape
    nt, _, ft = w1p.shape
    nd = w2r.shape[0]
    nr = 8
    rb = t // nr
    cfg = (nt, nr, rb, ft, d, nd)
    return pl.pallas_call(
        functools.partial(kernel_a, cfg),
        out_shape=(jax.ShapeDtypeStruct((nt, t, ft), F32), jax.ShapeDtypeStruct((t, d), BF16),
                   jax.ShapeDtypeStruct((d, t), BF16), jax.ShapeDtypeStruct((d, t), BF16)),
        in_specs=[HBM] * 3, out_specs=(HBM,) * 4,
        scratch_shapes=[
            pltpu.VMEM((t, d), BF16), pltpu.VMEM((t, d), F32), pltpu.VMEM((2, t, ft), F32),
            pltpu.VMEM((2, d, ft), BF16), pltpu.VMEM((2, nd, ft // nd, d), BF16),
            pltpu.VMEM((rb, ft), BF16), pltpu.VMEM((rb, ft), BF16),
            pltpu.VMEM((2, rb, d), BF16), pltpu.VMEM((2, 2, d, rb), BF16),
            pltpu.SemaphoreType.DMA((1,)), pltpu.SemaphoreType.DMA((4,)),
            pltpu.SemaphoreType.DMA((2,)), pltpu.SemaphoreType.DMA((6,))],
        compiler_params=pltpu.CompilerParams(vmem_limit_bytes=64 * 1024 * 1024 - 65536),
        name="forward_one",
    )(x, w1p, w2r)


MESH = pl.DeviceIdType.MESH

def gelu_pair(pre):
    normal_cdf = 0.5 * (1.0 + lax.erf(pre * ROOT_HALF))
    density = jnp.exp(-0.5 * pre * pre) * INV_ROOT_TAU
    return pre * normal_cdf, normal_cdf + pre * density

def flip(value, step):
    return value + step * (1 - 2 * lax.rem(lax.div(value, step), 2))

ORDERS = ((0, 2, 1), (1, 2, 0))

def kernel_bc(cfg, u_hbm, ut_hbm, e_hbm, xt_hbm, z_hbm, w3_hbm, w4_hbm, w2_hbm,
              gu_hbm, gd_hbm, nrm_ref,
              act, actt, e_v, euacc, wa, wb, zb0, zb1, eb0, eb1, ht0, ht1, q0, q1,
              gu, gd, r0u, r0d, au, ad, r1u, r1d, r2u, r2d, r3u, r3d, fu, fd, nu, nd_acc, nsend, nrecv,
              insem, wsem, zsem, ssem, rsem, fsem, nsem):
    nt, nr, rb, ft, d, nd = cfg
    total = 2 * nt
    me = lax.axis_index("data")
    core = lax.rem(me, 2)
    chip = lax.div(me, 2)
    bits = [lax.rem(lax.div(chip, 1 << k), 2) for k in range(3)]
    partner = flip(me, 1)
    zb, eb, htb, qb = (zb0, zb1), (eb0, eb1), (ht0, ht1), (q0, q1)
    G, R, ACC, FIN, NRM, OUT = (gu, gd), ((r0u, r1u, r2u, r3u), (r0d, r1d, r2d, r3d)), (au, ad), (fu, fd), (nu, nd_acc), (gu_hbm, gd_hbm)

    loads = [pltpu.make_async_copy(u_hbm, act, insem.at[0]), pltpu.make_async_copy(ut_hbm, actt, insem.at[1]),
             pltpu.make_async_copy(e_hbm, e_v, insem.at[2])]
    for c in loads:
        c.start()

    def wcopies(j, slot, back):
        second = w2_hbm if back else w4_hbm
        cps = [pltpu.make_async_copy(second.at[:, j], wb.at[slot], wsem.at[2 + slot])]
        if not back:
            cps.append(pltpu.make_async_copy(w3_hbm.at[j], wa.at[slot], wsem.at[slot]))
        return cps
    for c in wcopies(0, 0, False):
        c.start()

    barrier = pltpu.get_barrier_semaphore()
    for k in range(1, nd):
        pl.semaphore_signal(barrier, inc=1, device_id=(lax.rem(me + k, nd),), device_id_type=MESH)
    pl.semaphore_wait(barrier, nd - 1)

    nu[...] = jnp.zeros_like(nu)
    nd_acc[...] = jnp.zeros_like(nd_acc)
    def zero(r, _):
        euacc[pl.ds(pl.multiple_of(r * rb, rb), rb), :] = jnp.zeros((rb, d), F32)
        return 0
    lax.fori_loop(0, nr, zero, 0)

    def owner_chip(kind, p):
        out = 0
        for place, axis in enumerate(ORDERS[kind]):
            bit = bits[axis] if not (p >> (2 - place)) & 1 else 1 - bits[axis]
            out = out + bit * (1 << axis)
        return out

    def send(kind, stage, j):
        two = lax.rem(j, 2)
        four = lax.rem(j, 4)
        sem = (kind * 4 + stage) * 2 + two
        if stage == 0:
            src, dst, dev = G[kind].at[two, :, 1 - core], R[kind][0].at[two], partner
        else:
            lo = 8 >> stage
            src, dst = ACC[kind].at[four, pl.ds(lo, lo)], R[kind][stage].at[two]
            dev = flip(me, 2 << ORDERS[kind][stage - 1])
        return pltpu.make_async_remote_copy(src_ref=src, dst_ref=dst, send_sem=ssem.at[sem], recv_sem=rsem.at[sem],
                                            device_id=(dev,), device_id_type=MESH)

    def final_copy(kind, j):
        two = lax.rem(j, 2)
        return pltpu.make_async_copy(FIN[kind].at[two], OUT[kind].at[j], fsem.at[kind * 2 + two])

    def when_valid(j, fn):
        @pl.when(jnp.logical_and(j >= 0, j < total))
        def _():
            fn(j)

    def comm(step):
        def stage3(j):
            two, four = lax.rem(j, 2), lax.rem(j, 4)
            for kind in range(2):
                @pl.when(j >= 2)
                def _():
                    final_copy(kind, j - 2).wait()
                send(kind, 3, j).wait()
                f = (ACC[kind][four, 0] + R[kind][3][two, 0]) * (1.0 / nd)
                FIN[kind][two] = f
                NRM[kind][...] += f * f
            for kind in range(2):
                final_copy(kind, j).start()
        def stage2(j):
            two, four = lax.rem(j, 2), lax.rem(j, 4)
            for kind in range(2):
                send(kind, 2, j).wait()
                ACC[kind][four, 0:2] += R[kind][2][two]
            for kind in range(2):
                send(kind, 3, j).start()
        def stage1(j):
            two, four = lax.rem(j, 2), lax.rem(j, 4)
            for kind in range(2):
                send(kind, 1, j).wait()
                ACC[kind][four, 0:4] += R[kind][1][two]
            for kind in range(2):
                send(kind, 2, j).start()
        def stage0(j):
            two, four = lax.rem(j, 2), lax.rem(j, 4)
            for kind in range(2):
                send(kind, 0, j).wait()
                for p in range(8):
                    oc = owner_chip(kind, p)
                    ACC[kind][four, p] = G[kind][two, oc, core] + R[kind][0][two, oc]
            for kind in range(2):
                send(kind, 1, j).start()
        def start(j):
            for kind in range(2):
                send(kind, 0, j).start()
        when_valid(step - 5, stage3)
        when_valid(step - 4, stage2)
        when_valid(step - 3, stage1)
        when_valid(step - 2, stage0)
        when_valid(step - 1, start)

    def add_grads(slot, first, upd_u, upd_d):
        bu, bd = upd_u.reshape(gu.shape[1:]), upd_d.reshape(gd.shape[1:])
        gu[slot] = bu if first else gu[slot] + bu
        gd[slot] = bd if first else gd[slot] + bd

    for c in loads:
        c.wait()

    def tile_b(j, _):
        slot = lax.rem(j, 2)
        comm(j)
        for c in wcopies(j, slot, False):
            c.wait()
        @pl.when(j + 1 < nt)
        def _():
            for c in wcopies(j + 1, 1 - slot, False):
                c.start()
        def front(r):
            rows = pl.ds(r * rb, rb)
            zb[r % 2][...] = dot_nn(act[rows, :], wa[slot])
            eb[r % 2][...] = dot_nt(e_v[rows, :], wb[slot].reshape(ft, d)).astype(BF16)
        def middle(r):
            h, der = gelu_pair(zb[r % 2][...])
            htb[r % 2][...] = h.astype(BF16).T
            qb[r % 2][...] = (eb[r % 2][...].astype(F32) * der).astype(BF16)
        def back(r):
            rows = pl.ds(r * rb, rb)
            q = qb[r % 2][...]
            euacc[rows, :] += dot_nt(q, wa[slot])
            add_grads(slot, r == 0, dot_nn(actt[:, rows], q), dot_nn(htb[r % 2][...], e_v[rows, :]))
        front(0)
        for r in range(nr):
            middle(r)
            if r + 1 < nr:
                front(r + 1)
            if r >= 1:
                back(r - 1)
        back(nr - 1)
        return 0
    lax.fori_loop(0, nt, tile_b, 0)

    xt_in = pltpu.make_async_copy(xt_hbm, actt, insem.at[1])
    xt_in.start()
    for c in wcopies(0, nt % 2, True):
        c.start()
    def cast(r, _):
        rows = pl.ds(pl.multiple_of(r * rb, rb), rb)
        act[rows, :] = euacc[rows, :].astype(BF16)
        return 0
    lax.fori_loop(0, nr, cast, 0)
    def zcopy(j, slot):
        return pltpu.make_async_copy(z_hbm.at[j], euacc.at[:, pl.ds(pl.multiple_of(slot * ft, ft), ft)], zsem.at[slot])
    zcopy(0, nt % 2).start()
    xt_in.wait()

    def tile_c(step, _):
        j = step - nt
        slot = lax.rem(step, 2)
        comm(step)
        for c in wcopies(j, slot, True):
            c.wait()
        zcopy(j, slot).wait()
        @pl.when(j + 1 < nt)
        def _():
            for c in wcopies(j + 1, 1 - slot, True):
                c.start()
            zcopy(j + 1, 1 - slot).start()
        def front(r):
            rows = pl.ds(r * rb, rb)
            eb[r % 2][...] = dot_nt(act[rows, :], wb[slot].reshape(ft, d)).astype(BF16)
        def middle(r):
            rows = pl.ds(r * rb, rb)
            h, der = gelu_pair(euacc[rows, pl.ds(pl.multiple_of(slot * ft, ft), ft)])
            htb[r % 2][...] = h.astype(BF16).T
            qb[r % 2][...] = (eb[r % 2][...].astype(F32) * der).astype(BF16)
        def back(r):
            rows = pl.ds(r * rb, rb)
            add_grads(slot, r == 0, dot_nn(actt[:, rows], qb[r % 2][...]), dot_nn(htb[r % 2][...], act[rows, :]))
        front(0)
        for r in range(nr):
            middle(r)
            if r + 1 < nr:
                front(r + 1)
            if r >= 1:
                back(r - 1)
        back(nr - 1)
        return 0
    lax.fori_loop(nt, total, tile_c, 0)

    def drain(step, _):
        comm(step)
        return 0
    lax.fori_loop(total, total + 5, drain, 0)
    for kind in range(2):
        for j in (total - 2, total - 1):
            final_copy(kind, j).wait()

    part = jnp.zeros((8, 128), F32)
    for ref in (nu, nd_acc):
        rows, cols = ref.shape
        for a in range(rows // 8):
            for b in range(cols // 128):
                part = part + ref[8 * a:8 * a + 8, 128 * b:128 * b + 128]
    nsend[...] = part
    nrecv[me] = part
    for k in range(1, nd):
        pltpu.make_async_remote_copy(src_ref=nsend, dst_ref=nrecv.at[me], send_sem=nsem.at[0], recv_sem=nsem.at[1],
                                     device_id=(lax.rem(me + k, nd),), device_id_type=MESH).start()
    others = nrecv.at[pl.ds(0, nd - 1)]
    pltpu.make_async_remote_copy(src_ref=others, dst_ref=others, send_sem=nsem.at[0], recv_sem=nsem.at[1],
                                 device_id=(me,), device_id_type=MESH).wait()
    total_sq = nrecv[0]
    for k in range(1, nd):
        total_sq = total_sq + nrecv[k]
    nrm_ref[...] = total_sq

def backward(u, ut, e, xt, z, w3p, w4r, w2r):
    t, d = u.shape
    nt, _, ft = w3p.shape
    nd = w4r.shape[0]
    nr = 8
    rb = t // nr
    bu, bd = (d // nd, ft), (ft // nd, d)
    cfg = (nt, nr, rb, ft, d, nd)
    V = pltpu.VMEM
    scratch = [V((t, d), BF16), V((d, t), BF16), V((t, d), BF16), V((t, d), F32),
               V((2, d, ft), BF16), V((2, nd, ft // nd, d), BF16),
               V((rb, ft), F32), V((rb, ft), F32), V((rb, ft), BF16), V((rb, ft), BF16),
               V((ft, rb), BF16), V((ft, rb), BF16), V((rb, ft), BF16), V((rb, ft), BF16),
               V((2, 8, 2) + bu, F32), V((2, 8, 2) + bd, F32)]
    for n, c in ((2, 8), (4, 8), (2, 4), (2, 2), (2, 1)):
        scratch += [V((n, c) + bu, F32), V((n, c) + bd, F32)]
    scratch += [V((2,) + bu, F32), V((2,) + bd, F32), V(bu, F32), V(bd, F32), V((8, 128), F32), V((nd, 8, 128), F32)]
    D = pltpu.SemaphoreType.DMA
    scratch += [D((3,)), D((4,)), D((2,)), D((16,)), D((16,)), D((4,)), D((2,))]
    return pl.pallas_call(
        functools.partial(kernel_bc, cfg),
        out_shape=(jax.ShapeDtypeStruct((2 * nt,) + bu, F32), jax.ShapeDtypeStruct((2 * nt,) + bd, F32),
                   jax.ShapeDtypeStruct((8, 128), F32)),
        in_specs=[HBM] * 8, out_specs=(HBM, HBM, pl.BlockSpec(memory_space=pltpu.VMEM)),
        scratch_shapes=scratch,
        compiler_params=pltpu.CompilerParams(collective_id=0, has_side_effects=True, vmem_limit_bytes=64 * 1024 * 1024 - 65536),
        name="backward",
    )(u, ut, e, xt, z, w3p, w4r, w2r)

def kernel_permute(nd, nt, w1_ref, w3_ref, o1_ref, o3_ref):
    w = 16
    for src, dst in ((w1_ref, o1_ref), (w3_ref, o3_ref)):
        for j in range(nt):
            dst[j] = jnp.concatenate([src[:, (d * nt + j) * w:(d * nt + j + 1) * w] for d in range(nd)], axis=1)

def permute(w1, w3, nd, rows):
    d, f = w1.shape
    nt = f // (nd * 16)
    ft = nd * 16
    return pl.pallas_call(functools.partial(kernel_permute, nd, nt),
        grid=(d // rows,),
        in_specs=[pl.BlockSpec((rows, f), lambda i: (i, 0))] * 2,
        out_specs=[pl.BlockSpec((nt, rows, ft), lambda i: (0, i, 0))] * 2,
        out_shape=[jax.ShapeDtypeStruct((nt, d, ft), BF16)] * 2, name="permute")(w1, w3)


STEP = 20
BETA_ONE = 0.9
BETA_TWO = 0.95
EPSILON = 1e-8
NORM_EPS = 1e-6
CORR_ONE = 1.0 - BETA_ONE ** STEP
CORR_TWO = 1.0 - BETA_TWO ** STEP


def adam_step(grad_rows, master_old, mom_old, vel_old, clip_scale, learn_rate):
    scaled = clip_scale * grad_rows
    mom_new = BETA_ONE * mom_old + (1.0 - BETA_ONE) * scaled
    vel_new = BETA_TWO * vel_old + (1.0 - BETA_TWO) * scaled * scaled
    master_new = master_old - learn_rate * (mom_new / CORR_ONE) / (jnp.sqrt(vel_new / CORR_TWO) + EPSILON)
    return master_new.astype(jnp.bfloat16), master_new, mom_new, vel_new


def solution(mesh):
    groups = mesh.shape["data"]
    rows_spec = P("data", None)
    full_spec = P(None, None)
    scalar_spec = P()

    def shard_body(act_in, grad_out, w_up1, w_down1, w_up2, w_down2, master_up1, master_down1, master_up2, master_down2, mom_up1, mom_down1, mom_up2, mom_down2, vel_up1, vel_down1, vel_up2, vel_down2, learn_rate, clip_norm):
        ff, d = w_down1.shape
        nt = ff // (groups * 16)
        up1_tiles, up2_tiles = permute(w_up1, w_up2, groups, 64)
        down1_tiles = w_down1.reshape(groups, nt, 16, d)
        down2_tiles = w_down2.reshape(groups, nt, 16, d)
        pre1, mid, mid_t, in_t = forward_one(act_in, up1_tiles, down1_tiles)
        grads_up, grads_down, sq = backward(mid, mid_t, grad_out, in_t, pre1, up2_tiles, down2_tiles, down1_tiles)
        grad_norm = jnp.sqrt(jnp.sum(sq))
        clip_scale = jnp.minimum(1.0, clip_norm / (grad_norm + NORM_EPS))

        def up_rows(tiles):
            rows = tiles.shape[1]
            return tiles.reshape(nt, rows, groups, 16).transpose(1, 2, 0, 3).reshape(rows, ff)

        grad_list = (up_rows(grads_up[nt:]), grads_down[nt:].reshape(ff // groups, d), up_rows(grads_up[:nt]), grads_down[:nt].reshape(ff // groups, d))
        master_list = (master_up1, master_down1, master_up2, master_down2)
        mom_list = (mom_up1, mom_down1, mom_up2, mom_down2)
        vel_list = (vel_up1, vel_down1, vel_up2, vel_down2)
        layer_states = [adam_step(grad_list[layer_idx], master_list[layer_idx], mom_list[layer_idx], vel_list[layer_idx], clip_scale, learn_rate) for layer_idx in range(4)]
        new_weights = [lax.all_gather(layer_state[0], "data", axis=0, tiled=True) for layer_state in layer_states]
        results = new_weights
        for field_idx in range(1, 4):
            results = results + [layer_state[field_idx] for layer_state in layer_states]
        return tuple(results + [grad_norm])

    in_specs = (rows_spec, rows_spec) + (full_spec,) * 4 + (rows_spec,) * 12 + (scalar_spec, scalar_spec)
    out_specs = (full_spec,) * 4 + (rows_spec,) * 12 + (scalar_spec,)
    return jax.shard_map(shard_body, mesh=mesh, in_specs=in_specs, out_specs=out_specs, check_vma=False)
```

time: 1440 us -> 818 us (0.57)
  waiting for transfers between devices: 765 us -> 183 us
  Pallas kernels: 0 us -> 555 us
  matrix products: 537 us -> 0 us
  blocking collectives: 31.2 us -> 0 us
    reduce_scatter x4 -> x0, waiting for transfers between devices: 569 us -> none  [shard_body(): lax.psum_scatter(local_grad, 'data', scatter_dimension=0, tiled=True)]
    pallas_call x0 -> x3, Pallas kernels: none -> 555 us  [the longest x1 405 us: backward(): pl.pallas_call(functools.partial(kernel_bc, cfg), out_shape=(jax.ShapeDty...]
    dot_general x9 -> x0, matrix products: 491 us -> none  [the longest x3 173 us: mat_tn(): lax.dot_general(left, right, (((0,), (0,)), ((), ())), preferred_element_...]
    unnamed x1 -> x0, matrix products: 46.3 us -> none
    psum x1 -> x0, blocking collectives: 31.2 us -> none  [shard_body(): grad_norm = jnp.sqrt(lax.psum(local_sq, 'data'))]
    unnamed x19 -> x16, local copies, waits for them, and re-layouts: 53.1 us -> 30.7 us
  transfers between devices with their start and end apart: 8 -> 4, of which waited for: 8 -> 4; matrix products, arithmetic and copies ran while one was open for 13% -> 3% of each run, Pallas kernels for 0% -> 0%
where the time goes in v1:
time: 818 us; the launch traced here: 817 us
  Pallas kernels  555 us (68%)
  waiting for transfers between devices  183 us (22%)
  local copies, waits for them, and re-layouts  42.4 us (5%)
  other arithmetic  19.9 us (2%)
  between operations  17 us (2%)
    pallas_call x1, Pallas kernels, backward(): pl.pallas_call(functools.partial(kernel_bc, cfg), out_shape=(jax.ShapeDty...  405 us
    all_gather x4, waiting for transfers between devices, shard_body(): lax.all_gather(layer_state[0], 'data', axis=0, tiled=True)  183 us
    pallas_call x1, Pallas kernels, forward_one(): pl.pallas_call(functools.partial(kernel_a, cfg), out_shape=(jax.ShapeDtyp...  115 us
    pallas_call x1, Pallas kernels, permute(): pl.pallas_call(functools.partial(kernel_permute, nd, nt), grid=(d // rows...  34.8 us
    unnamed x16, local copies, waits for them, and re-layouts  30.7 us
  transfers between devices with their start and end apart: 4, of which 4 were waited for; matrix products, arithmetic and copies ran while one was open for 3% of the time, Pallas kernels for 0%

profile of v1, /device:TPU:0, one launch (start us, length us, event | category | flops | bytes accessed | tf_op | source)
XLA Modules:
  0.0 817.3 jit_solution(7369509508999389480)
XLA Ops:
  7.2 0.0 all-gather.11.cloned.1.call-start
  7.2 34.8 %permute.1 = (bf16[19,896,256]{2,1,0:T(8,128)(2,1)}, bf16[19,896,256]{2,1,0:T(8,128)(2,1)}) custom-call(bf16[896,4864]{1,0:T(8,128)(2,1)} %w1_ref.1, bf16[896,4864]{1,0:T(8,128)(2,1)} %w3_ref.1), custom_call_target="tpu_custom_call" | custom-call | tf_op jit(solution)/shard_map/permute/pallas_call | solution.py:409
  42.0 115.3 %forward_one.1 = (f32[19,4096,256]{2,1,0:T(8,128)}, bf16[4096,896]{1,0:T(8,128)(2,1)}, bf16[896,4096]{1,0:T(8,128)(2,1)}, bf16[896,4096]{1,0:T(8,128)(2,1)}) custom-call(bf16[4096,896]{1,0:T(8,128)(2,1)} %x_hbm.1, bf16[19,896,256]{2,1,0:T(8,128)(2,1)} %get-tuple-element.26.w1_hbm, bf16[16,19,16,896]{3,2,1,0:T(8,128)(2,1)} %bitcast.24), custom_call_target="tpu_custom_call" | custom-call | tf_op jit(solution)/shard_map/forward_one/pallas_call | solution.py:110
  157.3 405.0 %backward.1 = (f32[38,56,256]{2,1,0:T(8,128)}, f32[38,16,896]{2,1,0:T(8,128)}, f32[8,128]{1,0:T(8,128)}) custom-call(bf16[4096,896]{1,0:T(8,128)(2,1)} %get-tuple-element.27.u_hbm, bf16[896,4096]{1,0:T(8,128)(2,1)} %get-tuple-element.28.ut_hbm, bf16[4096,896]{1,0:T(8,128)(2,1)} %e_hbm.1, bf16[896,4096]{1,0:T(8,128)(2,1)} %get-tuple-element.29.xt_hbm, ...), custom_call_target="tpu_custom_call" | custom-call | tf_op jit(solution)/shard_map/backward/pallas_call | solution.py:389
  562.3 1.3 reduce_sum.9
  565.7 0.0 copy-start.1
  565.7 1.8 slice_multiply_fusion
  567.5 0.1 copy-done.1
  567.6 3.9 fusion.6
  571.5 0.0 all-gather.11.cloned.1.call-update
  571.5 0.0 all-gather.7.cloned.1.call-start
  571.5 0.0 copy-start
  571.6 4.4 fusion.11
  575.9 0.0 all-gather.7.cloned.1.call-update
  576.0 0.0 all-gather.9.cloned.1.call-start
  576.0 0.0 copy-done
  576.0 1.5 slice_multiply_fusion.1
  577.5 1.9 copy.80
  579.4 1.6 copy.81
  581.0 0.0 copy-start.2
  581.0 0.0 copy-start.3
  581.0 2.2 copy.82
  583.2 0.0 copy-done.2
  583.2 0.1 copy-done.3
  583.3 3.5 fusion.9
  586.9 0.0 all-gather.9.cloned.1.call-update
  586.9 0.0 all-gather.5.cloned.1.call-start
  586.9 2.1 copy.75
  589.1 1.6 copy.76
  590.7 0.0 copy-start.4
  590.7 0.0 copy-start.5
  590.7 2.2 copy.77
  592.9 0.0 copy-done.4
  592.9 0.1 copy-done.5
  593.0 3.5 fusion.14
  596.5 0.0 all-gather.5.cloned.1.call-update
  596.6 24.9 %all-gather.11.cloned.1.call-done = bf16[4864,896]{1,0:T(8,128)(2,1)} async-done(((bf16[304,896]{1,0:T(8,128)(2,1)}), bf16[4864,896]{1,0:T(8,128)(2,1)}) %all-gather.11.cloned.1.call-update) | async-done | bytes 8716304 | tf_op jit(solution)/shard_map/all_gather | solution.py:459
  621.5 52.6 %all-gather.7.cloned.1.call-done = bf16[4864,896]{1,0:T(8,128)(2,1)} async-done(((bf16[304,896]{1,0:T(8,128)(2,1)}), bf16[4864,896]{1,0:T(8,128)(2,1)}) %all-gather.7.cloned.1.call-update) | async-done | bytes 8716304 | tf_op jit(solution)/shard_map/all_gather | solution.py:459
  674.1 52.6 %all-gather.9.cloned.1.call-done = bf16[896,4864]{1,0:T(8,128)(2,1)} async-done(((bf16[56,4864]{1,0:T(8,128)(2,1)}), bf16[896,4864]{1,0:T(8,128)(2,1)}) %all-gather.9.cloned.1.call-update) | async-done | bytes 8716304 | tf_op jit(solution)/shard_map/all_gather | solution.py:459
  726.7 52.5 %all-gather.5.cloned.1.call-done = bf16[896,4864]{1,0:T(8,128)(2,1)} async-done(((bf16[56,4864]{1,0:T(8,128)(2,1)}), bf16[896,4864]{1,0:T(8,128)(2,1)}) %all-gather.5.cloned.1.call-update) | async-done | bytes 8716304 | tf_op jit(solution)/shard_map/all_gather | solution.py:459
  779.2 7.5 copy.91
  786.7 7.7 copy.92
  794.4 7.5 copy.93
  801.9 7.7 copy.94
Async XLA Ops:
  7.2 614.3 %all-gather.11.cloned.1.call-start = ((), (), s32[]{:S(2)}) async-start(), calls=%async_computation.3 | async-start | bytes 9261056 | tf_op jit(solution)/shard_map/all_gather | solution.py:459
  565.7 1.9 copy-start.1
  571.5 102.6 %all-gather.7.cloned.1.call-start = ((), (), s32[]{:S(2)}) async-start(), calls=%async_computation.1 | async-start | bytes 9261056 | tf_op jit(solution)/shard_map/all_gather | solution.py:459
  571.5 4.5 copy-start
  576.0 150.7 %all-gather.9.cloned.1.call-start = ((), (), s32[]{:S(2)}) async-start(), calls=%async_computation.2 | async-start | bytes 9261056 | tf_op jit(solution)/shard_map/all_gather | solution.py:459
  581.0 2.2 copy-start.2
  581.0 2.3 copy-start.3
  586.9 192.3 %all-gather.5.cloned.1.call-start = ((), (), s32[]{:S(2)}) async-start(), calls=%async_computation | async-start | bytes 9261056 | tf_op jit(solution)/shard_map/all_gather | solution.py:459
  590.7 2.2 copy-start.4
  590.7 2.3 copy-start.5
Sparse Core Ops, SparseCore 0:
  571.6 49.8 all-gather.10
  624.3 49.7 all-gather.6
  676.9 49.7 all-gather.8
  729.4 49.7 all-gather.4

commit v2 on v1

v2 whole, which is shorter than its diff:
```python
import functools
import math
import jax
import jax.numpy as jnp
from jax import lax
from jax.experimental import pallas as pl
from jax.experimental.pallas import tpu as pltpu
from jax.sharding import PartitionSpec as P

ROOT_HALF = math.sqrt(0.5)
INV_ROOT_TAU = 1.0 / math.sqrt(2.0 * math.pi)
F32, BF16 = jnp.float32, jnp.bfloat16
HBM = pl.BlockSpec(memory_space=pltpu.HBM)
VMEM_MAX = 64 * 1024 * 1024 - 65536
BLOCKS = 8


def dot_nn(a, b):
    return lax.dot_general(a, b, (((1,), (0,)), ((), ())), preferred_element_type=F32)


def dot_nt(a, b):
    return lax.dot_general(a, b, (((1,), (1,)), ((), ())), preferred_element_type=F32)


def gelu(z):
    return z * (0.5 * (1.0 + lax.erf(z * ROOT_HALF)))


def kernel_a(cfg, x_hbm, w1_hbm, w3_hbm, w2_hbm, z_hbm, u_hbm, ut_hbm, xt_hbm, w3p_hbm,
             x_v, uacc, zout, w1_v, w3_v, w1, w3, w2, h0, h1, sq, sqt, xsem, wsem, zsem, osem):
    nt, nr, rb, ft, d, nd = cfg
    hb = (h0, h1)
    step16 = ft // nd
    loads = [pltpu.make_async_copy(w1_hbm, w1_v, xsem.at[0]), pltpu.make_async_copy(x_hbm, x_v, xsem.at[1]),
             pltpu.make_async_copy(w3_hbm, w3_v, xsem.at[2])]
    for c in loads:
        c.start()

    def w2copy(j, slot):
        return pltpu.make_async_copy(w2_hbm.at[:, j], w2.at[slot], wsem.at[slot])

    def w3copy(j, slot):
        return pltpu.make_async_copy(w3.at[slot], w3p_hbm.at[j], wsem.at[2 + slot])

    def zcopy(j, slot):
        return pltpu.make_async_copy(zout.at[slot], z_hbm.at[j], zsem.at[slot])

    def xtcopy(r):
        return pltpu.make_async_copy(sqt, xt_hbm.at[:, pl.ds(pl.multiple_of(r * rb, rb), rb)], osem.at[0])
    w2copy(0, 0).start()

    lanes = 128
    per = lanes // step16
    group = lax.broadcasted_iota(jnp.int32, (d, lanes), 1) // step16

    def permute(src, dst, j, slot):
        for half in range(nd // per):
            acc = None
            for k in range(per // 2):
                pair = []
                for q in (k, k + per // 2):
                    place = nt * (half * per + q) + j
                    col = pl.multiple_of(lax.div(place, per) * lanes, lanes)
                    pair.append((src[:, pl.ds(col, lanes)], lax.rem(place, per)))
                mixed = jnp.where(group == pair[0][1], pair[0][0], pair[1][0])
                shift = lax.rem(k - pair[0][1] + per, per) * step16
                turned = pltpu.roll(mixed, shift, 1)
                acc = turned if acc is None else jnp.where(lax.rem(group, per // 2) == k, turned, acc)
            dst[slot, :, half * lanes:(half + 1) * lanes] = acc

    def zero(r, _):
        uacc[pl.ds(pl.multiple_of(r * rb, rb), rb), :] = jnp.zeros((rb, d), F32)
        return 0
    lax.fori_loop(0, nr, zero, 0)
    loads[0].wait()
    permute(w1_v, w1, 0, 0)
    loads[1].wait()
    loads[2].wait()

    def tile(j, _):
        slot = lax.rem(j, 2)
        nslot = 1 - slot
        xr = lax.rem(j, nr)
        @pl.when(j >= 2)
        def _():
            zcopy(j - 2, slot).wait()
            w3copy(j - 2, slot).wait()
        @pl.when(jnp.logical_and(j >= 1, j <= nr))
        def _():
            xtcopy(j - 1).wait()
        w2copy(j, slot).wait()
        @pl.when(j + 1 < nt)
        def _():
            w2copy(j + 1, nslot).start()
        def front(r):
            rows = pl.ds(r * rb, rb)
            zout[slot, rows, :] = dot_nn(x_v[rows, :], w1[slot])
        def middle(r):
            hb[r % 2][...] = gelu(zout[slot, pl.ds(r * rb, rb), :]).astype(BF16)
        def back(r):
            uacc[pl.ds(r * rb, rb), :] += dot_nn(hb[r % 2][...], w2[slot].reshape(ft, d))
        front(0)
        for r in range(nr):
            middle(r)
            if r + 1 < nr:
                front(r + 1)
            if r >= 1:
                back(r - 1)
            if r == 1:
                permute(w1_v, w1, jnp.minimum(j + 1, nt - 1), nslot)
            if r == 3:
                permute(w3_v, w3, j, slot)
            if r == 5:
                sqt[...] = x_v[pl.ds(pl.multiple_of(xr * rb, rb), rb), :].T
        back(nr - 1)
        zcopy(j, slot).start()
        w3copy(j, slot).start()
        @pl.when(j < nr)
        def _():
            xtcopy(j).start()
        return 0
    lax.fori_loop(0, nt, tile, 0)
    if nt <= nr:
        xtcopy(nt - 1).wait()
        for r in range(nt, nr):
            sqt[...] = x_v[pl.ds(r * rb, rb), :].T
            xtcopy(r).start()
            xtcopy(r).wait()

    def fin(r, _):
        rows = pl.ds(pl.multiple_of(r * rb, rb), rb)
        x_v[rows, :] = uacc[rows, :].astype(BF16)
        pltpu.make_async_copy(x_v.at[rows, :], u_hbm.at[rows, :], osem.at[1]).start()
        return 0
    lax.fori_loop(0, nr, fin, 0)
    def fin_t(r, _):
        rows = pl.ds(pl.multiple_of(r * rb, rb), rb)
        sq[r] = x_v[rows, :].T
        pltpu.make_async_copy(sq.at[r], ut_hbm.at[:, rows], osem.at[2]).start()
        return 0
    lax.fori_loop(0, nr, fin_t, 0)
    pltpu.make_async_copy(x_v, u_hbm, osem.at[1]).wait()
    pltpu.make_async_copy(ut_hbm, ut_hbm, osem.at[2]).wait()
    for j in (nt - 2, nt - 1):
        zcopy(j, j % 2).wait()
        w3copy(j, j % 2).wait()


def forward_one(x, w1, w3, w2r):
    t, d = x.shape
    nd, nt, rows2, _ = w2r.shape
    ft, nr = nd * rows2, BLOCKS
    rb = t // nr
    V, D = pltpu.VMEM, pltpu.SemaphoreType.DMA
    S = jax.ShapeDtypeStruct
    return pl.pallas_call(
        functools.partial(kernel_a, (nt, nr, rb, ft, d, nd)),
        out_shape=(S((nt, t, ft), F32), S((t, d), BF16), S((d, t), BF16), S((d, t), BF16), S((nt, d, ft), BF16)),
        in_specs=[HBM] * 4, out_specs=(HBM,) * 5,
        scratch_shapes=[
            V((t, d), BF16), V((t, d), F32), V((2, t, ft), F32), V(w1.shape, BF16), V(w3.shape, BF16),
            V((2, d, ft), BF16), V((2, d, ft), BF16), V((2, nd, rows2, d), BF16),
            V((rb, ft), BF16), V((rb, ft), BF16), V((nr, d, rb), BF16), V((d, rb), BF16),
            D((3,)), D((4,)), D((2,)), D((3,))],
        compiler_params=pltpu.CompilerParams(vmem_limit_bytes=VMEM_MAX),
        name="forward_one",
    )(x, w1, w3, w2r)


MESH = pl.DeviceIdType.MESH

def gelu_pair(pre):
    normal_cdf = 0.5 * (1.0 + lax.erf(pre * ROOT_HALF))
    density = jnp.exp(-0.5 * pre * pre) * INV_ROOT_TAU
    return pre * normal_cdf, normal_cdf + pre * density

def flip(value, step):
    return value + step * (1 - 2 * lax.rem(lax.div(value, step), 2))

def relative(kind, p, bits):
    out = 0
    for place, axis in enumerate(reversed(ORDERS[kind])):
        out = out + (1 - bits[axis] if (p >> place) & 1 else bits[axis]) * (1 << axis)
    return out


def position():
    me = lax.axis_index("data")
    chip = lax.div(me, 2)
    return me, lax.rem(me, 2), [lax.rem(lax.div(chip, 1 << k), 2) for k in range(3)]


ORDERS = ((0, 2, 1), (1, 2, 0))
PARTS = 8
SEEN = (2, 4, 6, 7)
DEPTH = (2, 4, 4, 2)
LAST = len(SEEN) - 1
ACCS = 5

def kernel_bc(cfg, u_hbm, ut_hbm, e_hbm, xt_hbm, z_hbm, w3_hbm, w4_hbm, w2_hbm,
              gu_hbm, gd_hbm, nrm_ref,
              act, actt, e_v, euacc, wa, wb, zb0, zb1, eb0, eb1, ht0, ht1, q0, q1,
              gu, gd, r0u, r0d, au, ad, r1u, r1d, r2u, r2d, r3u, r3d, fu, fd, nu, nd_acc, nsend, nrecv,
              insem, wsem, zsem, ssem, rsem, fsem, nsem):
    nt, nr, rb, ft, d, nd = cfg
    total = 2 * nt
    me, core, bits = position()
    partner = flip(me, 1)
    zb, eb, htb, qb = (zb0, zb1), (eb0, eb1), (ht0, ht1), (q0, q1)
    G, R, ACC, FIN, NRM, OUT = (gu, gd), ((r0u, r1u, r2u, r3u), (r0d, r1d, r2d, r3d)), (au, ad), (fu, fd), (nu, nd_acc), (gu_hbm, gd_hbm)

    loads = [pltpu.make_async_copy(u_hbm, act, insem.at[0]), pltpu.make_async_copy(ut_hbm, actt, insem.at[1]),
             pltpu.make_async_copy(e_hbm, e_v, insem.at[2])]
    for c in loads:
        c.start()

    def wcopies(j, slot, back):
        second = w2_hbm if back else w4_hbm
        cps = [pltpu.make_async_copy(second.at[:, j], wb.at[slot], wsem.at[1, slot])]
        if not back:
            cps.append(pltpu.make_async_copy(w3_hbm.at[j], wa.at[slot], wsem.at[0, slot]))
        return cps
    for c in wcopies(0, 0, False):
        c.start()

    barrier = pltpu.get_barrier_semaphore()
    for k in range(1, nd):
        pl.semaphore_signal(barrier, inc=1, device_id=(lax.rem(me + k, nd),), device_id_type=MESH)
    pl.semaphore_wait(barrier, nd - 1)

    nu[...] = jnp.zeros_like(nu)
    nd_acc[...] = jnp.zeros_like(nd_acc)
    def zero(r, _):
        euacc[pl.ds(pl.multiple_of(r * rb, rb), rb), :] = jnp.zeros((rb, d), F32)
        return 0
    lax.fori_loop(0, nr, zero, 0)

    def owner_chip(kind, p):
        return relative(kind, p, bits)

    def send(kind, stage, j):
        depth = R[kind][stage].shape[0]
        slot = lax.rem(j, depth)
        sem = (kind * len(SEEN) + stage) * max(DEPTH) + slot
        dst = R[kind][stage].at[slot]
        if stage == 0:
            src, dev = G[kind].at[slot, :, 1 - core], partner
        else:
            lo = PARTS >> stage
            src, dev = ACC[kind].at[lax.rem(j, ACCS), pl.ds(lo, lo)], flip(me, 2 << ORDERS[kind][stage - 1])
        return pltpu.make_async_remote_copy(src_ref=src, dst_ref=dst, send_sem=ssem.at[sem], recv_sem=rsem.at[sem],
                                            device_id=(dev,), device_id_type=MESH)

    def final_copy(kind, j):
        slot = lax.rem(j, 2)
        return pltpu.make_async_copy(FIN[kind].at[slot], OUT[kind].at[j], fsem.at[kind, slot])

    def absorb(stage, j):
        place = lax.rem(j, ACCS)
        for kind in range(2):
            send(kind, stage, j).wait()
            slot = lax.rem(j, R[kind][stage].shape[0])
            got, acc = R[kind][stage], ACC[kind]
            if stage == 0:
                for p in range(PARTS):
                    oc = owner_chip(kind, p)
                    acc[place, p] = G[kind][slot, oc, core] + got[slot, oc]
            elif stage < LAST:
                keep = pl.ds(0, PARTS >> stage)
                acc[place, keep] += got[slot]
            else:
                @pl.when(j >= 2)
                def _():
                    final_copy(kind, j - 2).wait()
                f = (acc[place, 0] + got[slot, 0]) * (1.0 / nd)
                FIN[kind][lax.rem(j, 2)] = f
                NRM[kind][...] += f * f
        for kind in range(2):
            (send(kind, stage + 1, j) if stage < LAST else final_copy(kind, j)).start()

    def comm(step):
        def when_valid(j, fn):
            @pl.when(jnp.logical_and(j >= 0, j < total))
            def _():
                fn()
        for stage in reversed(range(len(SEEN))):
            when_valid(step - SEEN[stage], functools.partial(absorb, stage, step - SEEN[stage]))
        def start():
            for kind in range(2):
                send(kind, 0, step - 1).start()
        when_valid(step - 1, start)

    def add_grads(slot, first, upd_u, upd_d):
        bu, bd = upd_u.reshape(gu.shape[1:]), upd_d.reshape(gd.shape[1:])
        gu[slot] = bu if first else gu[slot] + bu
        gd[slot] = bd if first else gd[slot] + bd

    for c in loads:
        c.wait()

    def tile_b(j, _):
        slot = lax.rem(j, 2)
        comm(j)
        for c in wcopies(j, slot, False):
            c.wait()
        @pl.when(j + 1 < nt)
        def _():
            for c in wcopies(j + 1, 1 - slot, False):
                c.start()
        def front(r):
            rows = pl.ds(r * rb, rb)
            zb[r % 2][...] = dot_nn(act[rows, :], wa[slot])
            eb[r % 2][...] = dot_nt(e_v[rows, :], wb[slot].reshape(ft, d)).astype(BF16)
        def middle(r):
            h, der = gelu_pair(zb[r % 2][...])
            htb[r % 2][...] = h.astype(BF16).T
            qb[r % 2][...] = (eb[r % 2][...].astype(F32) * der).astype(BF16)
        def back(r):
            rows = pl.ds(r * rb, rb)
            q = qb[r % 2][...]
            euacc[rows, :] += dot_nt(q, wa[slot])
            add_grads(slot, r == 0, dot_nn(actt[:, rows], q), dot_nn(htb[r % 2][...], e_v[rows, :]))
        front(0)
        for r in range(nr):
            middle(r)
            if r + 1 < nr:
                front(r + 1)
            if r >= 1:
                back(r - 1)
        back(nr - 1)
        return 0
    lax.fori_loop(0, nt, tile_b, 0)

    xt_in = pltpu.make_async_copy(xt_hbm, actt, insem.at[1])
    xt_in.start()
    for c in wcopies(0, nt % 2, True):
        c.start()
    def cast(r, _):
        rows = pl.ds(pl.multiple_of(r * rb, rb), rb)
        act[rows, :] = euacc[rows, :].astype(BF16)
        return 0
    lax.fori_loop(0, nr, cast, 0)
    def zcopy(j, slot):
        return pltpu.make_async_copy(z_hbm.at[j], euacc.at[:, pl.ds(pl.multiple_of(slot * ft, ft), ft)], zsem.at[slot])
    zcopy(0, nt % 2).start()
    xt_in.wait()

    def tile_c(step, _):
        j = step - nt
        slot = lax.rem(step, 2)
        comm(step)
        for c in wcopies(j, slot, True):
            c.wait()
        zcopy(j, slot).wait()
        @pl.when(j + 1 < nt)
        def _():
            for c in wcopies(j + 1, 1 - slot, True):
                c.start()
            zcopy(j + 1, 1 - slot).start()
        def front(r):
            rows = pl.ds(r * rb, rb)
            eb[r % 2][...] = dot_nt(act[rows, :], wb[slot].reshape(ft, d)).astype(BF16)
        def middle(r):
            rows = pl.ds(r * rb, rb)
            h, der = gelu_pair(euacc[rows, pl.ds(pl.multiple_of(slot * ft, ft), ft)])
            htb[r % 2][...] = h.astype(BF16).T
            qb[r % 2][...] = (eb[r % 2][...].astype(F32) * der).astype(BF16)
        def back(r):
            rows = pl.ds(r * rb, rb)
            add_grads(slot, r == 0, dot_nn(actt[:, rows], qb[r % 2][...]), dot_nn(htb[r % 2][...], act[rows, :]))
        front(0)
        for r in range(nr):
            middle(r)
            if r + 1 < nr:
                front(r + 1)
            if r >= 1:
                back(r - 1)
        back(nr - 1)
        return 0
    lax.fori_loop(nt, total, tile_c, 0)

    def drain(step, _):
        comm(step)
        return 0
    lax.fori_loop(total, total + SEEN[LAST], drain, 0)
    for kind in range(2):
        for j in (total - 2, total - 1):
            final_copy(kind, j).wait()

    part = jnp.zeros((8, 128), F32)
    for ref in (nu, nd_acc):
        rows, cols = ref.shape
        for a in range(rows // 8):
            for b in range(cols // 128):
                part = part + ref[8 * a:8 * a + 8, 128 * b:128 * b + 128]
    nsend[...] = part
    nrecv[me] = part
    for k in range(1, nd):
        pltpu.make_async_remote_copy(src_ref=nsend, dst_ref=nrecv.at[me], send_sem=nsem.at[0], recv_sem=nsem.at[1],
                                     device_id=(lax.rem(me + k, nd),), device_id_type=MESH).start()
    others = nrecv.at[pl.ds(0, nd - 1)]
    pltpu.make_async_remote_copy(src_ref=others, dst_ref=others, send_sem=nsem.at[0], recv_sem=nsem.at[1],
                                 device_id=(me,), device_id_type=MESH).wait()
    total_sq = nrecv[0]
    for k in range(1, nd):
        total_sq = total_sq + nrecv[k]
    nrm_ref[...] = total_sq

def backward(u, ut, e, xt, z, w3p, w4r, w2r):
    t, d = u.shape
    nt, _, ft = w3p.shape
    nd = w4r.shape[0]
    nr = 8
    rb = t // nr
    bu, bd = (d // nd, ft), (ft // nd, d)
    cfg = (nt, nr, rb, ft, d, nd)
    V = pltpu.VMEM
    scratch = [V((t, d), BF16), V((d, t), BF16), V((t, d), BF16), V((t, d), F32),
               V((2, d, ft), BF16), V((2, nd, ft // nd, d), BF16),
               V((rb, ft), F32), V((rb, ft), F32), V((rb, ft), BF16), V((rb, ft), BF16),
               V((ft, rb), BF16), V((ft, rb), BF16), V((rb, ft), BF16), V((rb, ft), BF16),
               V((2, 8, 2) + bu, F32), V((2, 8, 2) + bd, F32)]
    for n, c in ((DEPTH[0], PARTS), (ACCS, PARTS)) + tuple((DEPTH[k], PARTS >> k) for k in range(1, LAST + 1)):
        scratch += [V((n, c) + bu, F32), V((n, c) + bd, F32)]
    scratch += [V((2,) + bu, F32), V((2,) + bd, F32), V(bu, F32), V(bd, F32), V((8, 128), F32), V((nd, 8, 128), F32)]
    D = pltpu.SemaphoreType.DMA
    scratch += [D((3,)), D((2, 2)), D((2,)), D((2 * len(SEEN) * max(DEPTH),)), D((2 * len(SEEN) * max(DEPTH),)), D((2, 2)), D((2,))]
    return pl.pallas_call(
        functools.partial(kernel_bc, cfg),
        out_shape=(jax.ShapeDtypeStruct((2 * nt,) + bu, F32), jax.ShapeDtypeStruct((2 * nt,) + bd, F32),
                   jax.ShapeDtypeStruct((8, 128), F32)),
        in_specs=[HBM] * 8, out_specs=(HBM, HBM, pl.BlockSpec(memory_space=pltpu.VMEM)),
        scratch_shapes=scratch,
        compiler_params=pltpu.CompilerParams(collective_id=0, has_side_effects=True, vmem_limit_bytes=VMEM_MAX),
        name="backward",
    )(u, ut, e, xt, z, w3p, w4r, w2r)


LAG = 2

def kernel_gather(cfg, su, sd, ou, od, lsem, rsem, ssem, dsem):
    nd, np_, ru, cu, rd = cfg
    pieces = 2 * np_
    me, core, bits = position()
    partner = flip(me, 1)
    barrier = pltpu.get_barrier_semaphore()
    for peer in (partner, flip(me, 2), flip(me, 4), flip(me, 8)):
        pl.semaphore_signal(barrier, inc=1, device_id=(peer,), device_id_type=MESH)
    pl.semaphore_wait(barrier, 4)

    def owner(kind, p):
        return 2 * relative(kind, p, bits) + core

    def block(kind, who, j, ref, local=False):
        w, k = lax.div(j, np_), lax.rem(j, np_)
        if kind == 0:
            row = 0 if local else pl.multiple_of(who * ru, 8)
            return ref.at[w, pl.ds(row, ru), pl.ds(pl.multiple_of(k * cu, 128), cu)]
        row = k * rd if local else who * (rd * np_) + k * rd
        return ref.at[w, pl.ds(pl.multiple_of(row, 8), rd), :]

    IN, O = (su, sd), (ou, od)
    own = [pltpu.make_async_copy(su, ou.at[:, pl.ds(pl.multiple_of(me * ru, 8), ru), :], lsem.at[0]),
           pltpu.make_async_copy(sd, od.at[:, pl.ds(pl.multiple_of(me * (rd * np_), 8), rd * np_), :], lsem.at[1])]

    def push(kind, p, j, dev, send, recv):
        who = owner(kind, p)
        src = block(kind, who, j, IN[kind], True) if p == 0 else block(kind, who, j, O[kind])
        pltpu.make_async_remote_copy(src_ref=src, dst_ref=block(kind, who, j, O[kind]), send_sem=send, recv_sem=recv,
                                     device_id=(dev,), device_id_type=MESH).start()

    def spread(kind, stage, j):
        dev = flip(me, 2 << ORDERS[kind][2 - stage])
        slot = lax.rem(j, 2 * LAG)
        for p in range(1 << stage):
            push(kind, p, j, dev, ssem.at[kind * 3 + stage], rsem.at[(kind * 3 + stage) * 2 * LAG + slot])

    def local(kind, ps, j):
        for p in ps:
            push(kind, p, j, partner, dsem.at[kind], dsem.at[2 + kind])

    def arrived(kind, stage, j):
        n = 1 << stage
        slot = lax.rem(j, 2 * LAG)
        size = O[kind].at[0, pl.ds(0, n * ru), pl.ds(0, cu)] if kind == 0 else O[kind].at[0, pl.ds(0, n * rd), :]
        sem = rsem.at[(kind * 3 + stage) * 2 * LAG + slot]
        pltpu.make_async_remote_copy(src_ref=size, dst_ref=size, send_sem=sem, recv_sem=sem, device_id=(me,), device_id_type=MESH).wait_recv()

    def step(s, _):
        for stage in (3, 2, 1, 0):
            j = s - stage * LAG
            @pl.when(jnp.logical_and(j >= 0, j < pieces))
            def _():
                for kind in range(2):
                    if stage:
                        arrived(kind, stage - 1, j)
                    if stage < 3:
                        spread(kind, stage, j)
                    local(kind, range((1 << stage) >> 1, 1 << stage), j)
        return 0
    for c in own:
        c.start()
    lax.fori_loop(0, pieces + 3 * LAG, step, 0)
    for c in own:
        c.wait()
    for kind in range(2):
        full = O[kind].at[0]
        rows = O[kind].shape[1] // 8
        pltpu.make_async_remote_copy(src_ref=full, dst_ref=full, send_sem=dsem.at[kind], recv_sem=dsem.at[2 + kind], device_id=(me,), device_id_type=MESH).wait()
        for stage in range(3):
            part = O[kind].at[0, pl.ds(0, rows << stage)]
            pltpu.make_async_remote_copy(src_ref=part, dst_ref=part, send_sem=ssem.at[kind * 3 + stage], recv_sem=dsem.at[2 + kind], device_id=(me,), device_id_type=MESH).wait_send()

def gather(su, sd, nd):
    _, ru, f = su.shape
    _, rf, d = sd.shape
    np_ = rf // 16
    cfg = (nd, np_, ru, f // np_, 16)
    D = pltpu.SemaphoreType.DMA
    anyspec = pl.BlockSpec(memory_space=pl.ANY)
    return pl.pallas_call(functools.partial(kernel_gather, cfg),
        out_shape=(jax.ShapeDtypeStruct((2, ru * nd, f), BF16), jax.ShapeDtypeStruct((2, rf * nd, d), BF16)),
        in_specs=[anyspec] * 2, out_specs=(anyspec,) * 2,
        scratch_shapes=[D((2,)), D((12 * LAG,)), D((6,)), D((4,))],
        compiler_params=pltpu.CompilerParams(collective_id=1, has_side_effects=True, vmem_limit_bytes=1024 * 1024),
        name="gather")(su, sd)


STEP = 20
BETA_ONE = 0.9
BETA_TWO = 0.95
EPSILON = 1e-8
NORM_EPS = 1e-6
CORR_ONE = 1.0 - BETA_ONE ** STEP
CORR_TWO = 1.0 - BETA_TWO ** STEP


def kernel_adam(cfg, sq_ref, hyper_ref, gu_hbm, gd_hbm, *refs):
    nd, nt = cfg
    states, outs, (nu_ref, nd_ref, norm_ref), (gbuf_u, gbuf_d, sbuf_u, sbuf_d, obuf_u, obuf_d, lsem, osem) = refs[:12], refs[12:24], refs[24:27], refs[27:]
    lanes, width = 128, 16
    per = lanes // width
    gbuf, sbuf, obuf, half = (gbuf_u, gbuf_d), (sbuf_u, sbuf_d), (obuf_u, obuf_d), (nu_ref, nd_ref)
    order = (2, 3, 1, 0)

    def loads(k):
        kind, layer = k % 2, k // 2
        src = (gu_hbm, gd_hbm)[kind].at[pl.ds((1 - layer) * nt, nt)]
        return [pltpu.make_async_copy(src, gbuf[kind].at[layer], lsem.at[k])] + [
            pltpu.make_async_copy(states[4 * f + k], sbuf[kind].at[layer, f], lsem.at[k]) for f in range(3)]

    def stores(k):
        kind, layer = k % 2, k // 2
        return [pltpu.make_async_copy(obuf[kind].at[layer, f], outs[4 * f + k], osem.at[k]) for f in range(3)]
    for k in order:
        for c in loads(k):
            c.start()
    norm = jnp.sqrt(jnp.sum(sq_ref[...], keepdims=True))
    norm_ref[...] = norm
    rate, clip = hyper_ref[0], hyper_ref[1]
    scale = jnp.minimum(1.0, clip / (norm + NORM_EPS))
    group = lax.broadcasted_iota(jnp.int32, (8, lanes), 1) // width

    def update(kind, layer, rows, grad):
        master, mom, vel = [sbuf[kind][layer, f, rows, :] for f in range(3)]
        scaled = scale * grad
        mom = BETA_ONE * mom + (1.0 - BETA_ONE) * scaled
        vel = BETA_TWO * vel + (1.0 - BETA_TWO) * scaled * scaled
        master = master - rate * (mom * (1.0 / CORR_ONE)) / (jnp.sqrt(vel * (1.0 / CORR_TWO)) + EPSILON)
        half[kind][layer, rows, :] = master.astype(BF16)
        for f, value in enumerate((master, mom, vel)):
            obuf[kind][layer, f, rows, :] = value

    for k in order:
        kind, layer = k % 2, k // 2
        for c in loads(k):
            c.wait()
        if kind == 0:
            def body(r, _):
                rows = pl.ds(pl.multiple_of(r * 8, 8), 8)
                cols = []
                for t in range(nd * nt // per):
                    acc = None
                    for s in range(per):
                        k_owner, j = divmod(per * t + s, nt)
                        src = gbuf_u[layer, j, rows, (k_owner // per) * lanes:(k_owner // per + 1) * lanes]
                        shift = (s - k_owner) % per * width
                        turned = pltpu.roll(src, shift, 1) if shift else src
                        acc = turned if acc is None else jnp.where(group == s, turned, acc)
                    cols.append(acc)
                update(0, layer, rows, jnp.concatenate(cols, axis=1))
                return 0
            lax.fori_loop(0, sbuf_u.shape[2] // 8, body, 0)
        else:
            def body(j, _):
                n = gbuf_d.shape[2]
                update(1, layer, pl.ds(pl.multiple_of(j * n, n), n), gbuf_d[layer, j])
                return 0
            lax.fori_loop(0, nt, body, 0)
        for c in stores(k):
            c.start()
    for k in order:
        for c in stores(k):
            c.wait()


def adam(sq, hyper, gu, gd, states, nd):
    nt = gu.shape[0] // 2
    up, down = states[0].shape, states[1].shape
    S, V, D = jax.ShapeDtypeStruct, pltpu.VMEM, pltpu.SemaphoreType.DMA
    vm = pl.BlockSpec(memory_space=pltpu.VMEM)
    return pl.pallas_call(
        functools.partial(kernel_adam, (nd, nt)),
        out_shape=tuple(S(s.shape, F32) for s in states) + (S((2,) + up, BF16), S((2,) + down, BF16), S((1, 1), F32)),
        in_specs=[vm, pl.BlockSpec(memory_space=pltpu.SMEM)] + [HBM] * 14, out_specs=(HBM,) * 12 + (vm,) * 3,
        scratch_shapes=[V((2, nt) + gu.shape[1:], F32), V((2, nt) + gd.shape[1:], F32), V((2, 3) + up, F32), V((2, 3) + down, F32),
                        V((2, 3) + up, F32), V((2, 3) + down, F32), D((4,)), D((4,))],
        compiler_params=pltpu.CompilerParams(vmem_limit_bytes=VMEM_MAX),
        name="adam")(sq, hyper, gu, gd, *states)


def solution(mesh):
    groups = mesh.shape["data"]
    rows_spec = P("data", None)
    full_spec = P(None, None)
    scalar_spec = P()

    def shard_body(act_in, grad_out, w_up1, w_down1, w_up2, w_down2, *rest):
        states, learn_rate, clip_norm = rest[:12], rest[12], rest[13]
        ff, d = w_down1.shape
        down1_tiles = w_down1.reshape(groups, -1, 16, d)
        down2_tiles = w_down2.reshape(groups, -1, 16, d)
        pre1, mid, mid_t, in_t, up2_tiles = forward_one(act_in, w_up1, w_up2, down1_tiles)
        grads_up, grads_down, sq = backward(mid, mid_t, grad_out, in_t, pre1, up2_tiles, down2_tiles, down1_tiles)
        *new_states, up_half, down_half, norm = adam(sq, jnp.stack([learn_rate, clip_norm]), grads_up, grads_down, states, groups)
        up_full, down_full = gather(up_half, down_half, groups)
        return (up_full[0], down_full[0], up_full[1], down_full[1], *new_states, norm.reshape(()))

    in_specs = (rows_spec, rows_spec) + (full_spec,) * 4 + (rows_spec,) * 12 + (scalar_spec, scalar_spec)
    out_specs = (full_spec,) * 4 + (rows_spec,) * 12 + (scalar_spec,)
    return jax.shard_map(shard_body, mesh=mesh, in_specs=in_specs, out_specs=out_specs, check_vma=False)
```

time: 818 us -> 697 us (0.85)
  waiting for transfers between devices: 183 us -> 0 us
  Pallas kernels: 555 us -> 679 us
  local copies, waits for them, and re-layouts: 42.4 us -> 15.2 us
  other arithmetic: 19.9 us -> 0.59 us
  between operations: 17 us -> 1.99 us
    all_gather x4 -> x0, waiting for transfers between devices: 183 us -> none  [shard_body(): lax.all_gather(layer_state[0], 'data', axis=0, tiled=True)]
    pallas_call x2 -> x3, Pallas kernels: 150 us -> 271 us  [the longest x1 131 us: forward_one(): pl.pallas_call(functools.partial(kernel_a, (nt, nr, rb, ft, d, nd)), out_...]
    unnamed x16 -> x4, local copies, waits for them, and re-layouts: 30.7 us -> 2.47 us
    convert_element_type x4 -> x0, other arithmetic: 15.4 us -> none  [adam_step(): return (master_new.astype(jnp.bfloat16), master_new, mom_new, vel_new)]
    squeeze x0 -> x2, local copies, waits for them, and re-layouts: none -> 12.8 us  [the longest x1 6.43 us: shard_body(): down_full[1]]
    mul x6 -> x0, local copies, waits for them, and re-layouts: 11.7 us -> none  [adam_step(): scaled = clip_scale * grad_rows]
  transfers between devices with their start and end apart: 4 -> 0, of which waited for: 4 -> 0; matrix products, arithmetic and copies ran while one was open for 3% -> 0% of each run, Pallas kernels for 0% -> 0%
where the time goes in v2:
time: 697 us
  Pallas kernels  679 us (97%)
  local copies, waits for them, and re-layouts  15.2 us (2%)
    pallas_call x1, Pallas kernels, backward(): pl.pallas_call(functools.partial(kernel_bc, cfg), out_shape=(jax.ShapeDty...  409 us
    pallas_call x1, Pallas kernels, forward_one(): pl.pallas_call(functools.partial(kernel_a, (nt, nr, rb, ft, d, nd)), out_...  131 us
    pallas_call x1, Pallas kernels, gather(): pl.pallas_call(functools.partial(kernel_gather, cfg), out_shape=(jax.Shap...  125 us
    pallas_call x1, Pallas kernels, adam(): pl.pallas_call(functools.partial(kernel_adam, (nd, nt)), out_shape=tuple(...  14 us

profile of v2, /device:TPU:0, one launch (start us, length us, event | category | flops | bytes accessed | tf_op | source)
XLA Modules:
  0.0 697.1 jit_solution(16692313380245342600)
XLA Ops:
  0.7 131.2 %forward_one.1 = (f32[19,4096,256]{2,1,0:T(8,128)}, bf16[4096,896]{1,0:T(8,128)(2,1)}, bf16[896,4096]{1,0:T(8,128)(2,1)}, bf16[896,4096]{1,0:T(8,128)(2,1)}, bf16[19,896,256]{2,1,0:T(8,128)(2,1)}) custom-call(bf16[4096,896]{1,0:T(8,128)(2,1)} %x_hbm.1, bf16[896,4864]{1,0:T(8,128)(2,1)} %w1_hbm.1, bf16[896,4864]{1,0:T(8,128)(2,1)} %w3_hbm.1, ...), custom_call_target="tpu_custom_call" | custom-call | tf_op jit(solution)/shard_map/forward_one/pallas_call | solution.py:157
  131.9 408.6 %backward.1 = (f32[38,56,256]{2,1,0:T(8,128)}, f32[38,16,896]{2,1,0:T(8,128)}, f32[8,128]{1,0:T(8,128)}) custom-call(bf16[4096,896]{1,0:T(8,128)(2,1)} %get-tuple-element.42.u_hbm, bf16[896,4096]{1,0:T(8,128)(2,1)} %get-tuple-element.43.ut_hbm, bf16[4096,896]{1,0:T(8,128)(2,1)} %e_hbm.1, bf16[896,4096]{1,0:T(8,128)(2,1)} %get-tuple-element.44.xt_hbm, ...), custom_call_target="tpu_custom_call" | custom-call | tf_op jit(solution)/shard_map/backward/pallas_call | solution.py:429
  541.8 0.6 pad_maximum_fusion.hyper_ref
  542.4 14.0 %adam.1 = (f32[56,4864]{1,0:T(8,128)}, f32[304,896]{1,0:T(8,128)}, f32[56,4864]{1,0:T(8,128)}, f32[304,896]{1,0:T(8,128)}, f32[56,4864]{1,0:T(8,128)}, /*index=5...) custom-call(f32[8,128]{1,0:T(8,128)} %get-tuple-element.47.sq_ref, ...), custom_call_target="tpu_custom_call" | custom-call | tf_op jit(solution)/shard_map/adam/pallas_call | solution.py:613
  556.4 0.0 copy-start
  556.4 1.2 copy-done
  557.7 0.0 copy-start.1
  557.7 1.2 copy-done.1
  558.9 125.5 %gather.1 = (bf16[2,896,4864]{2,1,0:T(8,128)(2,1)S(1)}, bf16[2,4864,896]{2,1,0:T(8,128)(2,1)S(1)}) custom-call(bf16[2,56,4864]{2,1,0:T(8,128)(2,1)S(1)} %copy-done, bf16[2,304,896]{2,1,0:T(8,128)(2,1)S(1)} %copy-done.1), custom_call_target="tpu_custom_call" | custom-call | tf_op jit(solution)/shard_map/gather/pallas_call | solution.py:522
  684.4 6.4 slice_bitcast_fusion
  690.8 6.3 slice_bitcast_fusion.1
Async XLA Ops:
  556.4 1.2 copy-start
  557.7 1.2 copy-start.1

commit v3 on v2

--- a/solution.py
+++ b/solution.py
@@ -13,6 +13,7 @@
 HBM = pl.BlockSpec(memory_space=pltpu.HBM)
 VMEM_MAX = 64 * 1024 * 1024 - 65536
 BLOCKS = 8
+RING = 6
 
 
 def dot_nn(a, b):
@@ -27,80 +28,123 @@
     return z * (0.5 * (1.0 + lax.erf(z * ROOT_HALF)))
 
 
-def kernel_a(cfg, x_hbm, w1_hbm, w3_hbm, w2_hbm, z_hbm, u_hbm, ut_hbm, xt_hbm, w3p_hbm,
-             x_v, uacc, zout, w1_v, w3_v, w1, w3, w2, h0, h1, sq, sqt, xsem, wsem, zsem, osem):
+def at_most(j, bound):
+    return jnp.minimum(j, bound)
+
+
+def aligned(j, size):
+    return pl.ds(pl.multiple_of(j * size, size), size)
+
+
+def kernel_a(cfg, x_hbm, e_hbm, w1_hbm, w3_hbm, w2_hbm, z_hbm, ut_hbm, xt_hbm, et_hbm, w3t_hbm,
+             xt, uacc, zout, w1t_v, w1_in, x_in, w1, w2, w2t, w3_in, w3_out, e_in, e_out, h0, h1,
+             wsem, xsem, esem, vsem, zsem, osem):
     nt, nr, rb, ft, d, nd = cfg
     hb = (h0, h1)
-    step16 = ft // nd
-    loads = [pltpu.make_async_copy(w1_hbm, w1_v, xsem.at[0]), pltpu.make_async_copy(x_hbm, x_v, xsem.at[1]),
-             pltpu.make_async_copy(w3_hbm, w3_v, xsem.at[2])]
-    for c in loads:
+    width = ft // nd
+
+    def w1copy(q):
+        slot = lax.rem(q, RING)
+        return pltpu.make_async_copy(w1_hbm.at[:, aligned(q, ft)], w1_in.at[slot], wsem.at[slot])
+
+    def xcopy(r):
+        slot = lax.rem(r, RING)
+        return pltpu.make_async_copy(x_hbm.at[aligned(r, rb), :], x_in.at[slot], xsem.at[slot])
+
+    def w2copy(j):
+        slot = lax.rem(j, 2)
+        return pltpu.make_async_copy(w2_hbm.at[:, j], w2.at[slot], vsem.at[0, slot])
+
+    def w3copy(j):
+        slot = lax.rem(j, 2)
+        return pltpu.make_async_copy(w3_hbm.at[:, aligned(j, ft)], w3_in.at[slot], vsem.at[1, slot])
+
+    def w3store(j):
+        slot = lax.rem(j, 2)
+        return pltpu.make_async_copy(w3_out.at[slot], w3t_hbm.at[aligned(j, ft), :], osem.at[0, slot])
+
+    def ecopy(r):
+        slot = lax.rem(r, 2)
+        return pltpu.make_async_copy(e_hbm.at[aligned(r, rb), :], e_in.at[slot], esem.at[slot])
+
+    def estore(r):
+        slot = lax.rem(r, 2)
+        return pltpu.make_async_copy(e_out.at[slot], et_hbm.at[:, aligned(r, rb)], osem.at[1, slot])
+
+    def zstore(j):
+        slot = lax.rem(j, 2)
+        return pltpu.make_async_copy(zout.at[slot], z_hbm.at[j], zsem.at[slot])
+
+    for q in range(min(RING, nt)):
+        w1copy(q).start()
+    for r in range(min(RING, nr)):
+        xcopy(r).start()
+    for c in (w2copy(0), w3copy(0), ecopy(0)):
         c.start()
 
-    def w2copy(j, slot):
-        return pltpu.make_async_copy(w2_hbm.at[:, j], w2.at[slot], wsem.at[slot])
-
-    def w3copy(j, slot):
-        return pltpu.make_async_copy(w3.at[slot], w3p_hbm.at[j], wsem.at[2 + slot])
-
-    def zcopy(j, slot):
-        return pltpu.make_async_copy(zout.at[slot], z_hbm.at[j], zsem.at[slot])
-
-    def xtcopy(r):
-        return pltpu.make_async_copy(sqt, xt_hbm.at[:, pl.ds(pl.multiple_of(r * rb, rb), rb)], osem.at[0])
-    w2copy(0, 0).start()
-
-    lanes = 128
-    per = lanes // step16
-    group = lax.broadcasted_iota(jnp.int32, (d, lanes), 1) // step16
-
-    def permute(src, dst, j, slot):
-        for half in range(nd // per):
-            acc = None
-            for k in range(per // 2):
-                pair = []
-                for q in (k, k + per // 2):
-                    place = nt * (half * per + q) + j
-                    col = pl.multiple_of(lax.div(place, per) * lanes, lanes)
-                    pair.append((src[:, pl.ds(col, lanes)], lax.rem(place, per)))
-                mixed = jnp.where(group == pair[0][1], pair[0][0], pair[1][0])
-                shift = lax.rem(k - pair[0][1] + per, per) * step16
-                turned = pltpu.roll(mixed, shift, 1)
-                acc = turned if acc is None else jnp.where(lax.rem(group, per // 2) == k, turned, acc)
-            dst[slot, :, half * lanes:(half + 1) * lanes] = acc
-
     def zero(r, _):
-        uacc[pl.ds(pl.multiple_of(r * rb, rb), rb), :] = jnp.zeros((rb, d), F32)
+        uacc[:, aligned(r, rb)] = jnp.zeros((d, rb), F32)
         return 0
     lax.fori_loop(0, nr, zero, 0)
-    loads[0].wait()
-    permute(w1_v, w1, 0, 0)
-    loads[1].wait()
-    loads[2].wait()
+
+    def turn_w1(q, _):
+        w1copy(q).wait()
+        w1t_v[aligned(q, ft), :] = w1_in[lax.rem(q, RING)].T
+        @pl.when(q + RING < nt)
+        def _():
+            w1copy(q + RING).start()
+        return 0
+    lax.fori_loop(0, nt, turn_w1, 0)
+
+    def turn_x(r, _):
+        xcopy(r).wait()
+        xt[:, aligned(r, rb)] = x_in[lax.rem(r, RING)].T
+        @pl.when(r + RING < nr)
+        def _():
+            xcopy(r + RING).start()
+        return 0
+    lax.fori_loop(0, nr, turn_x, 0)
+    xt_store = pltpu.make_async_copy(xt, xt_hbm, osem.at[2, 0])
+    xt_store.start()
+
+    def pick_w1(j, slot):
+        for k in range(nd):
+            w1[slot, k * width:(k + 1) * width, :] = w1t_v[aligned(k * nt + j, width), :]
+    pick_w1(0, 0)
 
     def tile(j, _):
         slot = lax.rem(j, 2)
         nslot = 1 - slot
-        xr = lax.rem(j, nr)
         @pl.when(j >= 2)
         def _():
-            zcopy(j - 2, slot).wait()
-            w3copy(j - 2, slot).wait()
-        @pl.when(jnp.logical_and(j >= 1, j <= nr))
-        def _():
-            xtcopy(j - 1).wait()
-        w2copy(j, slot).wait()
+            zstore(j - 2).wait()
+            w3store(j - 2).wait()
+        @pl.when(jnp.logical_and(j >= 2, j < nr + 2))
+        def _():
+            estore(j - 2).wait()
+        w2copy(j).wait()
+        w3copy(j).wait()
+        @pl.when(j < nr)
+        def _():
+            ecopy(j).wait()
         @pl.when(j + 1 < nt)
         def _():
-            w2copy(j + 1, nslot).start()
+            w2copy(j + 1).start()
+            w3copy(j + 1).start()
+        @pl.when(j + 1 < min(nr, nt))
+        def _():
+            ecopy(j + 1).start()
+
+        def cols(r):
+            return pl.ds(r * rb, rb)
         def front(r):
-            rows = pl.ds(r * rb, rb)
-            zout[slot, rows, :] = dot_nn(x_v[rows, :], w1[slot])
+            zout[slot, :, cols(r)] = dot_nn(w1[slot], xt[:, cols(r)])
         def middle(r):
-            hb[r % 2][...] = gelu(zout[slot, pl.ds(r * rb, rb), :]).astype(BF16)
+            hb[r % 2][...] = gelu(zout[slot, :, cols(r)]).astype(BF16)
         def back(r):
-            uacc[pl.ds(r * rb, rb), :] += dot_nn(hb[r % 2][...], w2[slot].reshape(ft, d))
+            uacc[:, cols(r)] += dot_nn(w2t[...], hb[r % 2][...])
         front(0)
+        w2t[...] = w2[slot].reshape(ft, d).T
         for r in range(nr):
             middle(r)
             if r + 1 < nr:
@@ -108,46 +152,42 @@
             if r >= 1:
                 back(r - 1)
             if r == 1:
-                permute(w1_v, w1, jnp.minimum(j + 1, nt - 1), nslot)
+                pick_w1(at_most(j + 1, nt - 1), nslot)
             if r == 3:
-                permute(w3_v, w3, j, slot)
+                w3_out[slot] = w3_in[slot].T
             if r == 5:
-                sqt[...] = x_v[pl.ds(pl.multiple_of(xr * rb, rb), rb), :].T
+                e_out[slot] = e_in[slot].T
         back(nr - 1)
-        zcopy(j, slot).start()
-        w3copy(j, slot).start()
+        zstore(j).start()
+        w3store(j).start()
         @pl.when(j < nr)
         def _():
-            xtcopy(j).start()
+            estore(j).start()
         return 0
     lax.fori_loop(0, nt, tile, 0)
-    if nt <= nr:
-        xtcopy(nt - 1).wait()
-        for r in range(nt, nr):
-            sqt[...] = x_v[pl.ds(r * rb, rb), :].T
-            xtcopy(r).start()
-            xtcopy(r).wait()
-
-    def fin(r, _):
-        rows = pl.ds(pl.multiple_of(r * rb, rb), rb)
-        x_v[rows, :] = uacc[rows, :].astype(BF16)
-        pltpu.make_async_copy(x_v.at[rows, :], u_hbm.at[rows, :], osem.at[1]).start()
-        return 0
-    lax.fori_loop(0, nr, fin, 0)
-    def fin_t(r, _):
-        rows = pl.ds(pl.multiple_of(r * rb, rb), rb)
-        sq[r] = x_v[rows, :].T
-        pltpu.make_async_copy(sq.at[r], ut_hbm.at[:, rows], osem.at[2]).start()
-        return 0
-    lax.fori_loop(0, nr, fin_t, 0)
-    pltpu.make_async_copy(x_v, u_hbm, osem.at[1]).wait()
-    pltpu.make_async_copy(ut_hbm, ut_hbm, osem.at[2]).wait()
+    xt_store.wait()
+
+    def finish(r, _):
+        xt[:, aligned(r, rb)] = uacc[:, aligned(r, rb)].astype(BF16)
+        return 0
+    lax.fori_loop(0, nr, finish, 0)
+    ut_store = pltpu.make_async_copy(xt, ut_hbm, osem.at[2, 1])
+    ut_store.start()
     for j in (nt - 2, nt - 1):
-        zcopy(j, j % 2).wait()
-        w3copy(j, j % 2).wait()
-
-
-def forward_one(x, w1, w3, w2r):
+        zstore(j).wait()
+        w3store(j).wait()
+        if j < nr:
+            estore(j).wait()
+    for r in range(nt, nr):
+        ecopy(r).start()
+        ecopy(r).wait()
+        e_out[r % 2] = e_in[r % 2].T
+        estore(r).start()
+        estore(r).wait()
+    ut_store.wait()
+
+
+def forward_one(x, e, w1, w3, w2r):
     t, d = x.shape
     nd, nt, rows2, _ = w2r.shape
     ft, nr = nd * rows2, BLOCKS
@@ -156,16 +196,16 @@
     S = jax.ShapeDtypeStruct
     return pl.pallas_call(
         functools.partial(kernel_a, (nt, nr, rb, ft, d, nd)),
-        out_shape=(S((nt, t, ft), F32), S((t, d), BF16), S((d, t), BF16), S((d, t), BF16), S((nt, d, ft), BF16)),
-        in_specs=[HBM] * 4, out_specs=(HBM,) * 5,
+        out_shape=(S((nt, ft, t), F32), S((d, t), BF16), S((d, t), BF16), S((d, t), BF16), S((nt * ft, d), BF16)),
+        in_specs=[HBM] * 5, out_specs=(HBM,) * 5,
         scratch_shapes=[
-            V((t, d), BF16), V((t, d), F32), V((2, t, ft), F32), V(w1.shape, BF16), V(w3.shape, BF16),
-            V((2, d, ft), BF16), V((2, d, ft), BF16), V((2, nd, rows2, d), BF16),
-            V((rb, ft), BF16), V((rb, ft), BF16), V((nr, d, rb), BF16), V((d, rb), BF16),
-            D((3,)), D((4,)), D((2,)), D((3,))],
+            V((d, t), BF16), V((d, t), F32), V((2, ft, t), F32), V((nt * ft, d), BF16), V((RING, d, ft), BF16), V((RING, rb, d), BF16),
+            V((2, ft, d), BF16), V((2, nd, rows2, d), BF16), V((d, ft), BF16), V((2, d, ft), BF16), V((2, ft, d), BF16),
+            V((2, rb, d), BF16), V((2, d, rb), BF16), V((ft, rb), BF16), V((ft, rb), BF16),
+            D((RING,)), D((RING,)), D((2,)), D((2, 2)), D((2,)), D((3, 2))],
         compiler_params=pltpu.CompilerParams(vmem_limit_bytes=VMEM_MAX),
         name="forward_one",
-    )(x, w1, w3, w2r)
+    )(x, e, w1, w3, w2r)
 
 
 MESH = pl.DeviceIdType.MESH
@@ -193,25 +233,26 @@
 
 ORDERS = ((0, 2, 1), (1, 2, 0))
 PARTS = 8
-SEEN = (2, 4, 6, 7)
+BEGUN = 2
+TURN = 128
+SEEN = (3, 5, 7, 8)
 DEPTH = (2, 4, 4, 2)
 LAST = len(SEEN) - 1
 ACCS = 5
 
-def kernel_bc(cfg, u_hbm, ut_hbm, e_hbm, xt_hbm, z_hbm, w3_hbm, w4_hbm, w2_hbm,
+def kernel_bc(cfg, ut_hbm, et_hbm, xt_hbm, z_hbm, w3_hbm, w4_hbm, w2_hbm,
               gu_hbm, gd_hbm, nrm_ref,
-              act, actt, e_v, euacc, wa, wb, zb0, zb1, eb0, eb1, ht0, ht1, q0, q1,
-              gu, gd, r0u, r0d, au, ad, r1u, r1d, r2u, r2d, r3u, r3d, fu, fd, nu, nd_acc, nsend, nrecv,
+              act, side, euacc, wa, wb, wat, zb0, zb1, eb0, eb1, hb0, hb1, qb0, qb1,
+              gu, gt, gd, r0u, r0d, au, ad, r1u, r1d, r2u, r2d, r3u, r3d, fu, fd, nu, nd_acc, nsend, nrecv,
               insem, wsem, zsem, ssem, rsem, fsem, nsem):
     nt, nr, rb, ft, d, nd = cfg
     total = 2 * nt
     me, core, bits = position()
     partner = flip(me, 1)
-    zb, eb, htb, qb = (zb0, zb1), (eb0, eb1), (ht0, ht1), (q0, q1)
+    zb, eb, hb, qb = (zb0, zb1), (eb0, eb1), (hb0, hb1), (qb0, qb1)
     G, R, ACC, FIN, NRM, OUT = (gu, gd), ((r0u, r1u, r2u, r3u), (r0d, r1d, r2d, r3d)), (au, ad), (fu, fd), (nu, nd_acc), (gu_hbm, gd_hbm)
 
-    loads = [pltpu.make_async_copy(u_hbm, act, insem.at[0]), pltpu.make_async_copy(ut_hbm, actt, insem.at[1]),
-             pltpu.make_async_copy(e_hbm, e_v, insem.at[2])]
+    loads = [pltpu.make_async_copy(ut_hbm, act, insem.at[0]), pltpu.make_async_copy(et_hbm, side, insem.at[1])]
     for c in loads:
         c.start()
 
@@ -219,7 +260,7 @@
         second = w2_hbm if back else w4_hbm
         cps = [pltpu.make_async_copy(second.at[:, j], wb.at[slot], wsem.at[1, slot])]
         if not back:
-            cps.append(pltpu.make_async_copy(w3_hbm.at[j], wa.at[slot], wsem.at[0, slot]))
+            cps.append(pltpu.make_async_copy(w3_hbm.at[:, j], wa.at[slot], wsem.at[0, slot]))
         return cps
     for c in wcopies(0, 0, False):
         c.start()
@@ -231,8 +272,9 @@
 
     nu[...] = jnp.zeros_like(nu)
     nd_acc[...] = jnp.zeros_like(nd_acc)
+    gt[1] = jnp.zeros_like(gt[1])
     def zero(r, _):
-        euacc[pl.ds(pl.multiple_of(r * rb, rb), rb), :] = jnp.zeros((rb, d), F32)
+        euacc[:, aligned(r, rb)] = jnp.zeros((d, rb), F32)
         return 0
     lax.fori_loop(0, nr, zero, 0)
 
@@ -245,7 +287,7 @@
         sem = (kind * len(SEEN) + stage) * max(DEPTH) + slot
         dst = R[kind][stage].at[slot]
         if stage == 0:
-            src, dev = G[kind].at[slot, :, 1 - core], partner
+            src, dev = G[kind].at[lax.rem(j, G[kind].shape[0]), :, 1 - core], partner
         else:
             lo = PARTS >> stage
             src, dev = ACC[kind].at[lax.rem(j, ACCS), pl.ds(lo, lo)], flip(me, 2 << ORDERS[kind][stage - 1])
@@ -265,7 +307,7 @@
             if stage == 0:
                 for p in range(PARTS):
                     oc = owner_chip(kind, p)
-                    acc[place, p] = G[kind][slot, oc, core] + got[slot, oc]
+                    acc[place, p] = G[kind][lax.rem(j, G[kind].shape[0]), oc, core] + got[slot, oc]
             elif stage < LAST:
                 keep = pl.ds(0, PARTS >> stage)
                 acc[place, keep] += got[slot]
@@ -288,39 +330,29 @@
             when_valid(step - SEEN[stage], functools.partial(absorb, stage, step - SEEN[stage]))
         def start():
             for kind in range(2):
-                send(kind, 0, step - 1).start()
-        when_valid(step - 1, start)
-
-    def add_grads(slot, first, upd_u, upd_d):
-        bu, bd = upd_u.reshape(gu.shape[1:]), upd_d.reshape(gd.shape[1:])
-        gu[slot] = bu if first else gu[slot] + bu
-        gd[slot] = bd if first else gd[slot] + bd
-
-    for c in loads:
-        c.wait()
-
-    def tile_b(j, _):
-        slot = lax.rem(j, 2)
-        comm(j)
-        for c in wcopies(j, slot, False):
-            c.wait()
-        @pl.when(j + 1 < nt)
-        def _():
-            for c in wcopies(j + 1, 1 - slot, False):
-                c.start()
-        def front(r):
-            rows = pl.ds(r * rb, rb)
-            zb[r % 2][...] = dot_nn(act[rows, :], wa[slot])
-            eb[r % 2][...] = dot_nt(e_v[rows, :], wb[slot].reshape(ft, d)).astype(BF16)
-        def middle(r):
-            h, der = gelu_pair(zb[r % 2][...])
-            htb[r % 2][...] = h.astype(BF16).T
-            qb[r % 2][...] = (eb[r % 2][...].astype(F32) * der).astype(BF16)
-        def back(r):
-            rows = pl.ds(r * rb, rb)
-            q = qb[r % 2][...]
-            euacc[rows, :] += dot_nt(q, wa[slot])
-            add_grads(slot, r == 0, dot_nn(actt[:, rows], q), dot_nn(htb[r % 2][...], e_v[rows, :]))
+                send(kind, 0, step - BEGUN).start()
+        when_valid(step - BEGUN, start)
+
+    def cols(r):
+        return pl.ds(r * rb, rb)
+
+    def turn(step, part):
+        slot = lax.rem(step + 1, 2)
+        lanes = pl.ds(part * TURN, TURN)
+        gd[slot, :, :, :, lanes] = gt[slot, lanes, :].T.reshape(gd.shape[1:-1] + (TURN,))
+
+    def add_grads(step, r, up, down_t):
+        up = up.reshape(gu.shape[1:])
+        three, two = lax.rem(step, gu.shape[0]), lax.rem(step, 2)
+        gu[three] = up if r == 0 else gu[three] + up
+        gt[two] = down_t if r == 0 else gt[two] + down_t
+
+    def gates(r, pre):
+        h, der = gelu_pair(pre)
+        hb[r % 2][...] = h.astype(BF16)
+        qb[r % 2][...] = (eb[r % 2][...].astype(F32) * der).astype(BF16)
+
+    def pipeline(step, front, middle, back):
         front(0)
         for r in range(nr):
             middle(r)
@@ -328,21 +360,47 @@
                 front(r + 1)
             if r >= 1:
                 back(r - 1)
+            if r < d // TURN:
+                turn(step, r)
         back(nr - 1)
+
+    for c in loads:
+        c.wait()
+
+    def tile_b(j, _):
+        slot = lax.rem(j, 2)
+        comm(j)
+        for c in wcopies(j, slot, False):
+            c.wait()
+        @pl.when(j + 1 < nt)
+        def _():
+            for c in wcopies(j + 1, 1 - slot, False):
+                c.start()
+        def front(r):
+            zb[r % 2][...] = dot_nn(wa[slot].reshape(ft, d), act[:, cols(r)])
+            eb[r % 2][...] = dot_nn(wb[slot].reshape(ft, d), side[:, cols(r)]).astype(BF16)
+            if r == 0:
+                wat[...] = wa[slot].reshape(ft, d).T
+        def middle(r):
+            gates(r, zb[r % 2][...])
+        def back(r):
+            q = qb[r % 2][...]
+            euacc[:, cols(r)] += dot_nn(wat[...], q)
+            add_grads(j, r, dot_nt(act[:, cols(r)], q), dot_nt(side[:, cols(r)], hb[r % 2][...]))
+        pipeline(j, front, middle, back)
         return 0
     lax.fori_loop(0, nt, tile_b, 0)
 
-    xt_in = pltpu.make_async_copy(xt_hbm, actt, insem.at[1])
+    xt_in = pltpu.make_async_copy(xt_hbm, side, insem.at[1])
     xt_in.start()
     for c in wcopies(0, nt % 2, True):
         c.start()
     def cast(r, _):
-        rows = pl.ds(pl.multiple_of(r * rb, rb), rb)
-        act[rows, :] = euacc[rows, :].astype(BF16)
+        act[:, aligned(r, rb)] = euacc[:, aligned(r, rb)].astype(BF16)
         return 0
     lax.fori_loop(0, nr, cast, 0)
     def zcopy(j, slot):
-        return pltpu.make_async_copy(z_hbm.at[j], euacc.at[:, pl.ds(pl.multiple_of(slot * ft, ft), ft)], zsem.at[slot])
+        return pltpu.make_async_copy(z_hbm.at[j], euacc.at[aligned(slot, ft), :], zsem.at[slot])
     zcopy(0, nt % 2).start()
     xt_in.wait()
 
@@ -359,29 +417,21 @@
                 c.start()
             zcopy(j + 1, 1 - slot).start()
         def front(r):
-            rows = pl.ds(r * rb, rb)
-            eb[r % 2][...] = dot_nt(act[rows, :], wb[slot].reshape(ft, d)).astype(BF16)
+            eb[r % 2][...] = dot_nn(wb[slot].reshape(ft, d), act[:, cols(r)]).astype(BF16)
         def middle(r):
-            rows = pl.ds(r * rb, rb)
-            h, der = gelu_pair(euacc[rows, pl.ds(pl.multiple_of(slot * ft, ft), ft)])
-            htb[r % 2][...] = h.astype(BF16).T
-            qb[r % 2][...] = (eb[r % 2][...].astype(F32) * der).astype(BF16)
+            gates(r, euacc[aligned(slot, ft), cols(r)])
         def back(r):
-            rows = pl.ds(r * rb, rb)
-            add_grads(slot, r == 0, dot_nn(actt[:, rows], qb[r % 2][...]), dot_nn(htb[r % 2][...], act[rows, :]))
-        front(0)
-        for r in range(nr):
-            middle(r)
-            if r + 1 < nr:
-                front(r + 1)
-            if r >= 1:
-                back(r - 1)
-        back(nr - 1)
+            add_grads(step, r, dot_nt(side[:, cols(r)], qb[r % 2][...]), dot_nt(act[:, cols(r)], hb[r % 2][...]))
+        pipeline(step, front, middle, back)
         return 0
     lax.fori_loop(nt, total, tile_c, 0)
 
     def drain(step, _):
         comm(step)
+        @pl.when(step == total)
+        def _():
+            for part in range(d // TURN):
+                turn(step, part)
         return 0
     lax.fori_loop(total, total + SEEN[LAST], drain, 0)
     for kind in range(2):
@@ -407,34 +457,30 @@
         total_sq = total_sq + nrecv[k]
     nrm_ref[...] = total_sq
 
-def backward(u, ut, e, xt, z, w3p, w4r, w2r):
-    t, d = u.shape
-    nt, _, ft = w3p.shape
-    nd = w4r.shape[0]
-    nr = 8
+def backward(ut, et, xt, z, w3r, w4r, w2r):
+    d, t = ut.shape
+    nd, nt, rows2, _ = w4r.shape
+    ft, nr = nd * rows2, BLOCKS
     rb = t // nr
-    bu, bd = (d // nd, ft), (ft // nd, d)
-    cfg = (nt, nr, rb, ft, d, nd)
-    V = pltpu.VMEM
-    scratch = [V((t, d), BF16), V((d, t), BF16), V((t, d), BF16), V((t, d), F32),
-               V((2, d, ft), BF16), V((2, nd, ft // nd, d), BF16),
-               V((rb, ft), F32), V((rb, ft), F32), V((rb, ft), BF16), V((rb, ft), BF16),
-               V((ft, rb), BF16), V((ft, rb), BF16), V((rb, ft), BF16), V((rb, ft), BF16),
-               V((2, 8, 2) + bu, F32), V((2, 8, 2) + bd, F32)]
+    bu, bd = (d // nd, ft), (rows2, d)
+    V, D = pltpu.VMEM, pltpu.SemaphoreType.DMA
+    S = jax.ShapeDtypeStruct
+    scratch = [V((d, t), BF16)] * 2 + [V((d, t), F32)] + [V((2, nd, rows2, d), BF16)] * 2 + [V((d, ft), BF16)]
+    scratch += [V((ft, rb), F32)] * 2 + [V((ft, rb), BF16)] * 6
+    scratch += [V((3, PARTS, 2) + bu, F32), V((2, d, ft), F32), V((2, PARTS, 2) + bd, F32)]
     for n, c in ((DEPTH[0], PARTS), (ACCS, PARTS)) + tuple((DEPTH[k], PARTS >> k) for k in range(1, LAST + 1)):
         scratch += [V((n, c) + bu, F32), V((n, c) + bd, F32)]
     scratch += [V((2,) + bu, F32), V((2,) + bd, F32), V(bu, F32), V(bd, F32), V((8, 128), F32), V((nd, 8, 128), F32)]
-    D = pltpu.SemaphoreType.DMA
-    scratch += [D((3,)), D((2, 2)), D((2,)), D((2 * len(SEEN) * max(DEPTH),)), D((2 * len(SEEN) * max(DEPTH),)), D((2, 2)), D((2,))]
+    flags = 2 * len(SEEN) * max(DEPTH)
+    scratch += [D((2,)), D((2, 2)), D((2,)), D((flags,)), D((flags,)), D((2, 2)), D((2,))]
     return pl.pallas_call(
-        functools.partial(kernel_bc, cfg),
-        out_shape=(jax.ShapeDtypeStruct((2 * nt,) + bu, F32), jax.ShapeDtypeStruct((2 * nt,) + bd, F32),
-                   jax.ShapeDtypeStruct((8, 128), F32)),
-        in_specs=[HBM] * 8, out_specs=(HBM, HBM, pl.BlockSpec(memory_space=pltpu.VMEM)),
+        functools.partial(kernel_bc, (nt, nr, rb, ft, d, nd)),
+        out_shape=(S((2 * nt,) + bu, F32), S((2 * nt,) + bd, F32), S((8, 128), F32)),
+        in_specs=[HBM] * 7, out_specs=(HBM, HBM, pl.BlockSpec(memory_space=pltpu.VMEM)),
         scratch_shapes=scratch,
         compiler_params=pltpu.CompilerParams(collective_id=0, has_side_effects=True, vmem_limit_bytes=VMEM_MAX),
         name="backward",
-    )(u, ut, e, xt, z, w3p, w4r, w2r)
+    )(ut, et, xt, z, w3r, w4r, w2r)
 
 
 LAG = 2
@@ -631,8 +677,9 @@
         ff, d = w_down1.shape
         down1_tiles = w_down1.reshape(groups, -1, 16, d)
         down2_tiles = w_down2.reshape(groups, -1, 16, d)
-        pre1, mid, mid_t, in_t, up2_tiles = forward_one(act_in, w_up1, w_up2, down1_tiles)
-        grads_up, grads_down, sq = backward(mid, mid_t, grad_out, in_t, pre1, up2_tiles, down2_tiles, down1_tiles)
+        pre1, mid_t, in_t, grad_t, up2_t = forward_one(act_in, grad_out, w_up1, w_up2, down1_tiles)
+        up2_tiles = up2_t.reshape(down1_tiles.shape)
+        grads_up, grads_down, sq = backward(mid_t, grad_t, in_t, pre1, up2_tiles, down2_tiles, down1_tiles)
         *new_states, up_half, down_half, norm = adam(sq, jnp.stack([learn_rate, clip_norm]), grads_up, grads_down, states, groups)
         up_full, down_full = gather(up_half, down_half, groups)
         return (up_full[0], down_full[0], up_full[1], down_full[1], *new_states, norm.reshape(()))

time: 697 us -> 672 us (0.964)
  Pallas kernels: 679 us -> 642 us
  local copies, waits for them, and re-layouts: 15.2 us -> 26.6 us
    pallas_call x1, Pallas kernels: 131 us -> 101 us  [forward_one(): pl.pallas_call(functools.partial(kernel_a, (nt, nr, rb, ft, d, nd)), out_...]
    pallas_call x1, Pallas kernels: 409 us -> 401 us  [backward(): pl.pallas_call(functools.partial(kernel_bc, (nt, nr, rb, ft, d, nd)), out...]
where the time goes in v3:
time: 672 us; the launch traced here: 671 us
  Pallas kernels  642 us (96%)
  local copies, waits for them, and re-layouts  26.6 us (4%)
    pallas_call x1, Pallas kernels, backward(): pl.pallas_call(functools.partial(kernel_bc, (nt, nr, rb, ft, d, nd)), out...  401 us
    pallas_call x1, Pallas kernels, gather(): pl.pallas_call(functools.partial(kernel_gather, cfg), out_shape=(jax.Shap...  125 us
    pallas_call x1, Pallas kernels, forward_one(): pl.pallas_call(functools.partial(kernel_a, (nt, nr, rb, ft, d, nd)), out_...  101 us
    pallas_call x1, Pallas kernels, adam(): pl.pallas_call(functools.partial(kernel_adam, (nd, nt)), out_shape=tuple(...  14 us

profile of v3, /device:TPU:0, one launch (start us, length us, event | category | flops | bytes accessed | tf_op | source)
XLA Modules:
  0.0 670.9 jit_solution(10605743638930069463)
XLA Ops:
  0.7 101.2 %forward_one.1 = (f32[19,256,4096]{2,1,0:T(8,128)}, bf16[896,4096]{1,0:T(8,128)(2,1)}, bf16[896,4096]{1,0:T(8,128)(2,1)}, bf16[896,4096]{1,0:T(8,128)(2,1)}, bf16[4864,896]{1,0:T(8,128)(2,1)}) custom-call(bf16[4096,896]{1,0:T(8,128)(2,1)} %x_hbm.1, bf16[4096,896]{1,0:T(8,128)(2,1)} %e_hbm.1, bf16[896,4864]{1,0:T(8,128)(2,1)} %w1_hbm.1, ...), custom_call_target="tpu_custom_call" | custom-call | tf_op jit(solution)/shard_map/forward_one/pallas_call | solution.py:197
  101.9 401.1 %backward.1 = (f32[38,56,256]{2,1,0:T(8,128)}, f32[38,16,896]{2,1,0:T(8,128)}, f32[8,128]{1,0:T(8,128)}) custom-call(bf16[896,4096]{1,0:T(8,128)(2,1)} %get-tuple-element.42.ut_hbm, bf16[896,4096]{1,0:T(8,128)(2,1)} %get-tuple-element.43.et_hbm, bf16[896,4096]{1,0:T(8,128)(2,1)} %get-tuple-element.44.xt_hbm, f32[19,256,4096]{2,1,0:T(8,128)} %get-tuple-element.45.z_hbm, ...), custom_call_target="tpu_custom_call" | custom-call | tf_op jit(solution)/shard_map/backward/pallas_call | solution.py:476
  504.3 0.6 pad_maximum_fusion.hyper_ref
  504.9 14.0 %adam.1 = (f32[56,4864]{1,0:T(8,128)}, f32[304,896]{1,0:T(8,128)}, f32[56,4864]{1,0:T(8,128)}, f32[304,896]{1,0:T(8,128)}, f32[56,4864]{1,0:T(8,128)}, /*index=5...) custom-call(f32[8,128]{1,0:T(8,128)} %get-tuple-element.47.sq_ref, ...), custom_call_target="tpu_custom_call" | custom-call | tf_op jit(solution)/shard_map/adam/pallas_call | solution.py:659
  518.9 0.0 copy-start.1
  518.9 1.2 copy-done.1
  520.1 0.0 copy-start.2
  520.1 1.2 copy-done.2
  521.3 125.4 %gather.1 = (bf16[2,896,4864]{2,1,0:T(8,128)(2,1)S(1)}, bf16[2,4864,896]{2,1,0:T(8,128)(2,1)S(1)}) custom-call(bf16[2,56,4864]{2,1,0:T(8,128)(2,1)S(1)} %copy-done.1, bf16[2,304,896]{2,1,0:T(8,128)(2,1)S(1)} %copy-done.2), custom_call_target="tpu_custom_call" | custom-call | tf_op jit(solution)/shard_map/gather/pallas_call | solution.py:568
  646.8 0.0 copy-start
  646.8 5.9 copy-done
  652.7 11.9 %slice_bitcast_fusion = (bf16[4864,896]{1,0:T(8,128)(2,1)}, bf16[4864,896]{1,0:T(8,128)(2,1)}) fusion(bf16[2,4864,896]{2,1,0:T(8,128)(2,1)} %copy-done), kind=kLoop, calls=%fused_computation | loop fusion | bytes 34865152 | tf_op jit(solution)/shard_map/squeeze | solution.py:685
  664.6 6.3 slice_bitcast_fusion.1
Async XLA Ops:
  518.9 1.2 copy-start.1
  520.1 1.2 copy-start.2
  646.8 6.0 copy-start
